TPU v7x, 32 devices: a whole 2x2x4 slice. The times are simulated.
32 devices in a mesh: dp: 4 (over x, core), table: 8 (over z, y).
Axes of the slice: x: 2, y: 2, z: 4, core: 2. Of those that a mesh axis runs over, the one named last changes fastest.
Arguments:
- out_grad: bfloat16 [32768, 1024], P(('dp', 'table')), may hold values from -0.1875 to 0.1875
- pair_cells: int32 [32768, 8, 32], P(('dp', 'table')), may hold values from 0 to 4095
- weight_codes: int32 [32768, 8, 32], P(('dp', 'table')), may hold values from -127 to 127
- head_scale: float32 [8], replicated, may hold values from 0.5 to 2
- touch_slots: int32 [8, 8, 4], replicated, may hold values from 0 to 7
Outputs:
- grad_rows: bfloat16 [8192, 1024], P('table', 'dp')
All inputs are finite; a program needn't handle non-finite values.
Results may differ from a plain program's by a relative error of at most 0.0098.
Values may be sent and summed in bfloat16 or wider, within the bound.
No kernel may reach another device: no remote copies, remote signals or barrier semaphores. Data moves between devices by JAX's collectives and lax.ppermute only.
A program may use at most 128 MiB of HBM per device.

v0:
```python
import functools

import jax
import jax.numpy as jnp
from jax import lax
from jax.experimental import pallas as pl
from jax.experimental.pallas import tpu as pltpu
from jax.sharding import PartitionSpec as P


ROWS = 128
TOUCH = 32
OWN = 8
CELL_BITS = 12
CODE_BIAS = 128
BLOCK = 256
HALVES = 2
SIDE = 64
CHUNK_EDGES = (0, 2, 4, 8, 12, 16, 20, 24, 28, 32)
STAGE_EDGES = (0, 12, 20, 32)
LATE = 3


def fill_coef(scale_ref, cells_ref, codes_ref, write, low_ref, high_ref, weight_ref, table_ref):
    pairs, block = cells_ref.shape
    heads = scale_ref.shape[0]
    packed = (cells_ref[...] | ((codes_ref[...] + CODE_BIAS) << CELL_BITS)).T
    stride = table_ref.shape[0] // TOUCH
    tile = (packed >> 7) & (TOUCH - 1)
    upper = (packed >> 6) & 1
    low_ref[...] = (packed & (SIDE - 1)).astype(jnp.float32)
    high_ref[...] = (tile + TOUCH * upper).astype(jnp.float32)
    head = lax.broadcasted_iota(jnp.int32, (1, pairs), 1) // (pairs // heads)
    scale = jnp.zeros((1, pairs), jnp.float32)
    for h in range(heads):
        scale = jnp.where(head == h, scale_ref[h] / 128.0, scale)
    weight_ref[...] = ((packed >> CELL_BITS) - CODE_BIAS).astype(jnp.float32) * scale
    iota = lax.broadcasted_iota(jnp.int32, (SIDE, pairs), 0).astype(jnp.float32).astype(jnp.bfloat16)

    def spread(ref, token):
        row = jnp.broadcast_to(ref[pl.ds(token, 1), :], (16, pairs)).astype(jnp.bfloat16)
        return jnp.concatenate([row] * (SIDE // 16), axis=0)

    for token in range(block):
        low_hot = jnp.where(spread(low_ref, token) == iota, jnp.bfloat16(1), jnp.bfloat16(0))
        high_hot = jnp.where(spread(high_ref, token) == iota, spread(weight_ref, token), jnp.bfloat16(0))
        table = lax.dot_general(
            high_hot, low_hot, (((1,), (1,)), ((), ())), preferred_element_type=jnp.float32
        )
        table = jnp.concatenate([table[:TOUCH], table[TOUCH:]], axis=1)
        table_ref[pl.ds(token, TOUCH, stride=stride), :] = table
    for j in range(TOUCH):
        write(j, table_ref[pl.ds(j * stride, block), :].astype(jnp.bfloat16))


def distances(groups):
    half = groups // 2
    far, near = [n ^ 1 for n in range(half, groups)], list(range(half - 1, -1, -1))
    return far[:2] + near[:1] + far[2:3] + near[1:2] + far[3:] + near[2:]


def put_products(flip, coef, out_refs):
    product = jnp.dot(flip, coef, preferred_element_type=jnp.float32)
    for n, out_ref in enumerate(out_refs):
        width = out_ref.shape[1]
        for c in range(out_ref.shape[0]):
            part = product[n * width : (n + 1) * width, c * ROWS : (c + 1) * ROWS]
            out_ref[c] = part.astype(jnp.bfloat16)


def first_kernel(place_ref, scale_ref, cells_ref, codes_ref, *refs, groups):
    replicas = (len(refs) - 5 - 4 * HALVES) // 2
    grad_refs, (coef_hbm, flip_hbm) = refs[:replicas], refs[replicas : replicas + 2]
    out_refs = refs[replicas + 2 : 2 * replicas + 2]
    work_refs = refs[2 * replicas + 2 : -3]
    coef_ref, flip_ref, semaphores = refs[-3:]
    step = pl.program_id(0)
    block = cells_ref.shape[1]
    width = grad_refs[0].shape[1]
    blocks = coef_ref.shape[0] // block
    span = coef_ref.shape[1] // groups

    saves = [
        pltpu.make_async_copy(coef_ref, coef_hbm, semaphores.at[0]),
        pltpu.make_async_copy(flip_ref, flip_hbm, semaphores.at[1]),
    ]

    @pl.when(step < blocks)
    def _():
        rows = pl.ds(pl.multiple_of(step * block, block), block)
        for n in range(replicas):
            flip_ref[n * width : (n + 1) * width, rows] = grad_refs[n][...].T
        part = block // HALVES
        for half in range(HALVES):
            at = slice(half * part, (half + 1) * part)
            rows_of = pl.ds(pl.multiple_of(step * block + half * part, part), part)

            def write(j, value, rows_of=rows_of):
                coef_ref[rows_of, j * ROWS : (j + 1) * ROWS] = value

            fill_coef(
                scale_ref, cells_ref.at[:, at], codes_ref.at[:, at], write, *work_refs[4 * half : 4 * half + 4]
            )

    @pl.when(step >= blocks)
    def _():
        @pl.when(step == blocks)
        def _():
            for copy in saves:
                copy.start()

        owner = place_ref[2 + step - blocks]
        coef = coef_ref[:, pl.ds(pl.multiple_of(owner * span, span), span)]
        put_products(flip_ref[...], coef, out_refs)

    @pl.when(step == pl.num_programs(0) - 1)
    def _():
        for copy in saves:
            copy.wait()


def first_products(place, head_scale, cells, codes, grads, replicas, width, capacity, groups, length):
    pairs, tokens = cells.shape
    blocks = tokens // BLOCK
    last = blocks - 1
    spec = pl.BlockSpec((pairs, BLOCK), lambda i, *_: (0, jnp.minimum(i, last)))
    outs = [jax.ShapeDtypeStruct((length * capacity, width, ROWS), jnp.bfloat16) for _ in range(replicas)]
    cells_all = TOUCH * ROWS
    return pl.pallas_call(
        functools.partial(first_kernel, groups=groups),
        grid_spec=pltpu.PrefetchScalarGridSpec(
            num_scalar_prefetch=2,
            grid=(blocks + length,),
            in_specs=[spec, spec]
            + [
                pl.BlockSpec((BLOCK, width), lambda i, place, scale, m=m: (jnp.minimum(i, last), place[0] ^ m))
                for m in range(replicas)
            ],
            out_specs=[pl.BlockSpec(memory_space=pl.ANY), pl.BlockSpec(memory_space=pl.ANY)]
            + [
                pl.BlockSpec((capacity, width, ROWS), lambda i, *_: (jnp.maximum(i - blocks, 0), 0, 0))
                for _ in outs
            ],
            scratch_shapes=[
                pltpu.VMEM((BLOCK // HALVES, pairs), jnp.float32),
                pltpu.VMEM((BLOCK // HALVES, pairs), jnp.float32),
                pltpu.VMEM((BLOCK // HALVES, pairs), jnp.float32),
                pltpu.VMEM((TOUCH * (BLOCK // HALVES + 8), ROWS), jnp.float32),
            ]
            * HALVES
            + [
                pltpu.VMEM((tokens, cells_all), jnp.bfloat16),
                pltpu.VMEM((replicas * width, tokens), jnp.bfloat16),
                pltpu.SemaphoreType.DMA((2,)),
            ],
        ),
        out_shape=[
            jax.ShapeDtypeStruct((tokens, cells_all), jnp.bfloat16),
            jax.ShapeDtypeStruct((replicas * width, tokens), jnp.bfloat16),
        ]
        + outs,
        cost_estimate=pl.CostEstimate(
            flops=2 * tokens * pairs * cells_all * 4, transcendentals=0, bytes_accessed=tokens * cells_all * 4
        ),
        compiler_params=pltpu.CompilerParams(vmem_limit_bytes=22 << 20),
        name="first_products",
    )(place, pltpu.with_memory_space_constraint(head_scale, pltpu.HBM), *[pltpu.with_memory_space_constraint(a, pltpu.HBM) for a in [cells, codes] + [grads] * replicas])


def rest_kernel(place_ref, coef_ref, flip_ref, *refs, count):
    put_products(flip_ref[...], coef_ref[...], refs[-count:])


def rest_products(place, coef, flip, after, replicas, width, capacity, first, stop):
    tokens = coef.shape[0]
    length = stop - first
    return pl.pallas_call(
        functools.partial(rest_kernel, count=replicas),
        grid_spec=pltpu.PrefetchScalarGridSpec(
            num_scalar_prefetch=1,
            grid=(length,),
            in_specs=[
                pl.BlockSpec((tokens, capacity * ROWS), lambda i, place: (0, place[2 + first + i])),
                pl.BlockSpec(flip.shape, lambda i, place: (0, 0)),
                pl.BlockSpec(memory_space=pl.ANY),
            ],
            out_specs=[
                pl.BlockSpec((capacity, width, ROWS), lambda i, place: (i, 0, 0)) for _ in range(replicas)
            ],
        ),
        out_shape=[
            jax.ShapeDtypeStruct((length * capacity, width, ROWS), jnp.bfloat16) for _ in range(replicas)
        ],
        cost_estimate=pl.CostEstimate(
            flops=2 * tokens * length * capacity * ROWS * width * replicas,
            transcendentals=0,
            bytes_accessed=2 * length * capacity * ROWS * (tokens + replicas * width) + 2 * replicas * width * tokens,
        ),
        compiler_params=pltpu.CompilerParams(vmem_limit_bytes=12 << 20),
        name="rest_products",
    )(place, *[pltpu.with_memory_space_constraint(a, pltpu.VMEM) for a in (coef, flip)], after)


def add_kernel(*refs, plan):
    count = len(refs) - len(plan)
    for out_ref, terms in zip(refs[count:], plan):
        total = 0.0
        for n, at in terms:
            total = total + refs[n][at : at + out_ref.shape[0]].astype(jnp.float32)
        out_ref[...] = total.astype(jnp.bfloat16)


def add_tiles(sums, sizes):
    arrays = []
    plan = []
    for terms in sums:
        row = []
        for array, at in terms:
            known = [n for n, other in enumerate(arrays) if other is array]
            if not known:
                known = [len(arrays)]
                arrays.append(array)
            row.append((known[0], at))
        plan.append(tuple(row))
    spec = pl.BlockSpec(memory_space=pltpu.VMEM)
    return pl.pallas_call(
        functools.partial(add_kernel, plan=tuple(plan)),
        in_specs=[spec for _ in arrays],
        out_specs=[spec for _ in plan],
        out_shape=[pltpu.VMEM((size,) + arrays[0].shape[1:], jnp.bfloat16) for size in sizes],
        compiler_params=pltpu.CompilerParams(vmem_limit_bytes=4 << 20),
        name="add_tiles",
    )(*[pltpu.with_memory_space_constraint(array, pltpu.VMEM) for array in arrays])


def gather_kernel(place_ref, slot_ref, *refs, plan, first, last):
    refs = list(refs)
    sum_ref = refs.pop() if last else refs[-1]
    out_ref = refs.pop()
    owner = place_ref[1]
    if first:
        sum_ref[...] = jnp.zeros(sum_ref.shape, jnp.float32)
    else:
        sum_ref[...] = refs.pop(0)[...]
    for part_ref, (distance, at) in zip(refs, plan):
        for n in range(part_ref.shape[0]):
            slot = slot_ref[owner ^ distance, at + n, owner]
            sum_ref[slot] += part_ref[n].astype(jnp.float32)
    if last:
        for k in range(OWN):
            out_ref[pl.ds(k * ROWS, ROWS), :] = sum_ref[k].T.astype(jnp.bfloat16)


def gather_tiles(place, slots, parts, before=None, last=True):
    width = parts[0][2].shape[1]
    scalars = pl.BlockSpec(memory_space=pltpu.SMEM)
    spec = pl.BlockSpec(memory_space=pltpu.VMEM)
    arrays = [array for _, _, array in parts]
    if before is not None:
        arrays.insert(0, before)
    total = pltpu.VMEM((OWN, width, ROWS), jnp.float32)
    return pl.pallas_call(
        functools.partial(
            gather_kernel,
            plan=tuple((distance, at) for distance, at, _ in parts),
            first=before is None,
            last=last,
        ),
        in_specs=[scalars, scalars] + [spec for _ in arrays],
        out_specs=spec,
        scratch_shapes=[total] if last else [],
        out_shape=jax.ShapeDtypeStruct((OWN * ROWS, width), jnp.bfloat16) if last else total,
        compiler_params=pltpu.CompilerParams(vmem_limit_bytes=6 << 20),
        name="gather_tiles",
    )(place, slots, *[pltpu.with_memory_space_constraint(array, pltpu.VMEM) for array in arrays])


def body(out_grad, pair_cells, weight_codes, head_scale, touch_slots, *, replicas):
    tokens, value = out_grad.shape
    width = value // replicas
    groups = touch_slots.shape[0]
    capacity = touch_slots.shape[2]
    pairs = pair_cells.shape[1] * pair_cells.shape[2]
    order = distances(groups)
    owner = lax.axis_index("table")
    place = jnp.stack([lax.axis_index("dp"), owner] + [owner ^ n for n in order]).astype(jnp.int32)
    by_pair = lambda array: array.transpose(1, 2, 0).reshape(pairs, tokens)

    def swap(array, axis, bit):
        return lax.ppermute(array, axis, [(i, i ^ bit) for i in range(lax.axis_size(axis))])

    tiles = groups * capacity
    chunks = [(a * tiles // TOUCH, b * tiles // TOUCH) for a, b in zip(CHUNK_EDGES, CHUNK_EDGES[1:])]
    stages = [(a * tiles // TOUCH, b * tiles // TOUCH) for a, b in zip(STAGE_EDGES, STAGE_EDGES[1:])]
    pieces = [{m: [] for m in range(0, replicas, 2)} for _ in chunks]
    slots = touch_slots.transpose(0, 2, 1)
    sent = None
    for stage, (first, stop) in enumerate(stages):
        if stage == 0:
            coef, flip, *outs = first_products(
                place,
                head_scale,
                by_pair(pair_cells),
                by_pair(weight_codes),
                out_grad,
                replicas,
                width,
                capacity,
                groups,
                stop // capacity,
            )
        else:
            outs = rest_products(
                place, coef, flip, sent, replicas, width, capacity, first // capacity, stop // capacity
            )
        here = [n for n, (a, b) in enumerate(chunks) if first <= a < stop]
        sizes = [chunks[n][1] - chunks[n][0] for n in here]
        for m in sorted(range(replicas), reverse=True):
            array = swap(outs[m], "dp", 1) if m & 1 else outs[m]
            for n in here:
                pieces[n][m & ~1].append((array, chunks[n][0] - first))
        sent = outs[0]
        bit = 2
        while bit < replicas:
            masks = [m for m in sorted(pieces[here[0]], reverse=True) if m & bit]
            sums = add_tiles(
                [pieces[n].pop(m) for n in here for m in masks], [size for size in sizes for _ in masks]
            )
            sent = sums[0] if bit == 2 else sent
            sums = iter(sums)
            for n in here:
                for m in masks:
                    pieces[n][m ^ bit].append((swap(next(sums), "dp", bit), 0))
            bit *= 2
    parts = []
    for (a, b), piece in zip(chunks, pieces):
        (mine,) = add_tiles([piece[0]], [b - a])
        for start in range(a, b, min(capacity, b - a)):
            stop = min(start + capacity, b)
            distance = order[start // capacity]
            part = mine if stop - start == b - a else mine[start - a : stop - a]
            part = swap(part, "table", distance) if distance else part
            parts.append((distance, start % capacity, part))
    late = len(parts) - LATE
    total = gather_tiles(place, slots, parts[:late], last=False)
    return gather_tiles(place, slots, parts[late:], before=total)


def solution(mesh):
    return jax.shard_map(
        functools.partial(body, replicas=mesh.shape["dp"]),
        mesh=mesh,
        in_specs=(
            P(("dp", "table"), None),
            P(("dp", "table"), None, None),
            P(("dp", "table"), None, None),
            P(),
            P(),
        ),
        out_specs=P("table", "dp"),
        check_vma=False,
    )
```

profile of v0, /device:TPU:0, one launch (start us, length us, event | category | flops | bytes accessed | tf_op | source)
XLA Modules:
  0.0 103.7 jit_solution(7558123870004387131)
XLA Ops:
  0.0 0.1 stack.40.place_ref
  0.1 17.9 %first_products.1 = (bf16[1024,4096]{1,0:T(8,128)(2,1)S(1)}, bf16[1024,1024]{1,0:T(8,128)(2,1)S(1)}, bf16[12,256,128]{2,1,0:T(8,128)(2,1)S(1)}, bf16[12,256,128]...) custom-call(s32[10]{0:T(128)S(1)} %stack.40.place_ref, f32[8]{0:T(128)} %scale_ref.1, ...), custom_call_target="tpu_custom_call" | custom-call | flops 8589934592 | bytes 16777216 | tf_op jit(solution)/shard_map/first_products/pallas_call | solution.py:129
  18.0 0.6 collective-permute-start.1
  18.6 1.9 %collective-permute-done.1.refs_0_ = bf16[12,256,128]{2,1,0:T(8,128)(2,1)S(1)} collective-permute-done((bf16[12,256,128]{2,1,0:T(8,128)(2,1)S(1)}, bf16[12,256,128]{2,1,0:T(8,128)(2,1)S(1)}, u32[]{:S(2)}, u32[]{:S(2)}) %collective-permute-start.1) | collective-permute-done | bytes 786464 | tf_op jit(solution)/shard_map/ppermute | solution.py:290
  20.5 0.2 add_tiles.12
  20.7 3.3 %rest_products.2 = (bf16[8,256,128]{2,1,0:T(8,128)(2,1)S(1)}, bf16[8,256,128]{2,1,0:T(8,128)(2,1)S(1)}, bf16[8,256,128]{2,1,0:T(8,128)(2,1)S(1)}, bf16[8,256,128]{2,1,0:T(8,128)(2,1)S(1)}) custom-call(s32[10]{0:T(128)S(1)} %stack.40.place_ref, bf16[1024,4096]{1,0:T(8,128)(2,1)S(1)} %get-tuple-element.36.coef_ref, ...), custom_call_target="tpu_custom_call" | custom-call | flops 2147483648 | bytes 6291456 | tf_op jit(solution)/shard_map/rest_products/pallas_call | solution.py:177
  24.0 0.4 collective-permute-start.11
  24.4 0.1 collective-permute-start
  24.5 1.4 %collective-permute-done.11.refs_0_ = bf16[8,256,128]{2,1,0:T(8,128)(2,1)S(1)} collective-permute-done((bf16[8,256,128]{2,1,0:T(8,128)(2,1)S(1)}, bf16[8,256,128]{2,1,0:T(8,128)(2,1)S(1)}, u32[]{:S(2)}, u32[]{:S(2)}) %collective-permute-start.11) | collective-permute-done | bytes 524320 | tf_op jit(solution)/shard_map/ppermute | solution.py:290
  25.9 0.1 add_tiles.17
  26.1 4.6 %rest_products.3 = (bf16[12,256,128]{2,1,0:T(8,128)(2,1)S(1)}, bf16[12,256,128]{2,1,0:T(8,128)(2,1)S(1)}, bf16[12,256,128]{2,1,0:T(8,128)(2,1)S(1)}, bf16[12,256,128]{2,1,0:T(8,128)(2,1)S(1)}) custom-call(s32[10]{0:T(128)S(1)} %stack.40.place_ref, bf16[1024,4096]{1,0:T(8,128)(2,1)S(1)} %get-tuple-element.36.coef_ref, ...), custom_call_target="tpu_custom_call" | custom-call | flops 3221225472 | bytes 8388608 | tf_op jit(solution)/shard_map/rest_products/pallas_call | solution.py:177
  30.7 0.4 collective-permute-start.17
  31.1 0.1 collective-permute-start.16
  31.3 2.8 %collective-permute-start.2 = (bf16[2,256,128]{2,1,0:T(8,128)(2,1)S(1)}, bf16[2,256,128]{2,1,0:T(8,128)(2,1)S(1)}, u32[]{:S(2)}, u32[]{:S(2)}) collective-permute-start(bf16[2,256,128]{2,1,0:T(8,128)(2,1)S(1)} %get-tuple-element.32.refs_0_), channel_id=1, source_target_pairs={{0,16},{8,24},{16,0},{24,8},{1,17},{9,25},{17,1},{25,9},{2,18},{10... | collective-permute-start | bytes 393224 | tf_op jit(solution)/shard_map/ppermute | solution.py:290
  34.1 0.1 collective-permute-start.4
  34.3 4.2 %collective-permute-done.2.refs_2_ = bf16[2,256,128]{2,1,0:T(8,128)(2,1)S(1)} collective-permute-done((bf16[2,256,128]{2,1,0:T(8,128)(2,1)S(1)}, bf16[2,256,128]{2,1,0:T(8,128)(2,1)S(1)}, u32[]{:S(2)}, u32[]{:S(2)}) %collective-permute-start.2) | collective-permute-done | bytes 131104 | tf_op jit(solution)/shard_map/ppermute | solution.py:290
  38.5 2.0 %collective-permute-start.6 = (bf16[4,256,128]{2,1,0:T(8,128)(2,1)S(1)}, bf16[4,256,128]{2,1,0:T(8,128)(2,1)S(1)}, u32[]{:S(2)}, u32[]{:S(2)}) collective-permute-start(bf16[4,256,128]{2,1,0:T(8,128)(2,1)S(1)} %get-tuple-element.34), channel_id=1, source_target_pairs={{0,16},{8,24},{16,0},{24,8},{1,17},{9,25},{17,1},{25,9},{2,18},{10... | collective-permute-start | bytes 786440 | tf_op jit(solution)/shard_map/ppermute | solution.py:290
  40.5 0.8 collective-permute-done.4.refs_2_
  41.3 2.0 %collective-permute-start.8 = (bf16[4,256,128]{2,1,0:T(8,128)(2,1)S(1)}, bf16[4,256,128]{2,1,0:T(8,128)(2,1)S(1)}, u32[]{:S(2)}, u32[]{:S(2)}) collective-permute-start(bf16[4,256,128]{2,1,0:T(8,128)(2,1)S(1)} %get-tuple-element.35), channel_id=1, source_target_pairs={{0,16},{8,24},{16,0},{24,8},{1,17},{9,25},{17,1},{25,9},{2,18},{10... | collective-permute-start | bytes 786440 | tf_op jit(solution)/shard_map/ppermute | solution.py:290
  43.3 4.3 %collective-permute-done.6.refs_2_ = bf16[4,256,128]{2,1,0:T(8,128)(2,1)S(1)} collective-permute-done((bf16[4,256,128]{2,1,0:T(8,128)(2,1)S(1)}, bf16[4,256,128]{2,1,0:T(8,128)(2,1)S(1)}, u32[]{:S(2)}, u32[]{:S(2)}) %collective-permute-start.6) | collective-permute-done | bytes 262176 | tf_op jit(solution)/shard_map/ppermute | solution.py:290
  47.7 2.0 %collective-permute-start.12 = (bf16[4,256,128]{2,1,0:T(8,128)(2,1)S(1)}, bf16[4,256,128]{2,1,0:T(8,128)(2,1)S(1)}, u32[]{:S(2)}, u32[]{:S(2)}) collective-permute-start(bf16[4,256,128]{2,1,0:T(8,128)(2,1)S(1)} %get-tuple-element.42.refs_0_), channel_id=1, source_target_pairs={{0,16},{8,24},{16,0},{24,8},{1,17},{9,25},{17,1},{25,9},{2,18},{10... | collective-permute-start | bytes 786440 | tf_op jit(solution)/shard_map/ppermute | solution.py:290
  49.7 0.2 add_tiles.20
  49.9 3.4 %collective-permute-done.8.refs_2_ = bf16[4,256,128]{2,1,0:T(8,128)(2,1)S(1)} collective-permute-done((bf16[4,256,128]{2,1,0:T(8,128)(2,1)S(1)}, bf16[4,256,128]{2,1,0:T(8,128)(2,1)S(1)}, u32[]{:S(2)}, u32[]{:S(2)}) %collective-permute-start.8) | collective-permute-done | bytes 262176 | tf_op jit(solution)/shard_map/ppermute | solution.py:290
  53.3 2.0 %collective-permute-start.18 = (bf16[4,256,128]{2,1,0:T(8,128)(2,1)S(1)}, bf16[4,256,128]{2,1,0:T(8,128)(2,1)S(1)}, u32[]{:S(2)}, u32[]{:S(2)}) collective-permute-start(bf16[4,256,128]{2,1,0:T(8,128)(2,1)S(1)} %get-tuple-element.48), channel_id=1, source_target_pairs={{0,16},{8,24},{16,0},{24,8},{1,17},{9,25},{17,1},{25,9},{2,18},{10... | collective-permute-start | bytes 786440 | tf_op jit(solution)/shard_map/ppermute | solution.py:290
  55.3 0.1 add_tiles.15
  55.4 0.1 add_tiles.16
  55.5 3.4 %collective-permute-done.12.refs_2_ = bf16[4,256,128]{2,1,0:T(8,128)(2,1)S(1)} collective-permute-done((bf16[4,256,128]{2,1,0:T(8,128)(2,1)S(1)}, bf16[4,256,128]{2,1,0:T(8,128)(2,1)S(1)}, u32[]{:S(2)}, u32[]{:S(2)}) %collective-permute-start.12) | collective-permute-done | bytes 262176 | tf_op jit(solution)/shard_map/ppermute | solution.py:290
  58.9 3.1 %collective-permute-start.7 = (bf16[4,256,128]{2,1,0:T(8,128)(2,1)S(1)}, bf16[4,256,128]{2,1,0:T(8,128)(2,1)S(1)}, u32[]{:S(2)}, u32[]{:S(2)}) collective-permute-start(bf16[4,256,128]{2,1,0:T(8,128)(2,1)S(1)} %add_tiles.15), channel_id=1, source_target_pairs={{0,4},{1,5},{2,6},{3,7},{4,0},{5,1},{6,2},{7,3},{8,12},{9,13},{10,... | collective-permute-start | bytes 786440 | tf_op jit(solution)/shard_map/ppermute | solution.py:290
  62.0 2.5 %collective-permute-done.14.refs_2_ = bf16[4,256,128]{2,1,0:T(8,128)(2,1)S(1)} collective-permute-done((bf16[4,256,128]{2,1,0:T(8,128)(2,1)S(1)}, bf16[4,256,128]{2,1,0:T(8,128)(2,1)S(1)}, u32[]{:S(2)}, u32[]{:S(2)}) %collective-permute-start.14) | collective-permute-done | bytes 262176 | tf_op jit(solution)/shard_map/ppermute | solution.py:290
  64.5 3.1 %collective-permute-start.9 = (bf16[4,256,128]{2,1,0:T(8,128)(2,1)S(1)}, bf16[4,256,128]{2,1,0:T(8,128)(2,1)S(1)}, u32[]{:S(2)}, u32[]{:S(2)}) collective-permute-start(bf16[4,256,128]{2,1,0:T(8,128)(2,1)S(1)} %add_tiles.16), channel_id=1, source_target_pairs={{0,3},{1,2},{2,1},{3,0},{4,7},{5,6},{6,5},{7,4},{8,11},{9,10},{10,... | collective-permute-start | bytes 786440 | tf_op jit(solution)/shard_map/ppermute | solution.py:290
  67.6 0.1 add_tiles.14
  67.7 2.6 %collective-permute-start.3 = (bf16[2,256,128]{2,1,0:T(8,128)(2,1)S(1)}, bf16[2,256,128]{2,1,0:T(8,128)(2,1)S(1)}, u32[]{:S(2)}, u32[]{:S(2)}) collective-permute-start(bf16[2,256,128]{2,1,0:T(8,128)(2,1)S(1)} %add_tiles.13), channel_id=1, source_target_pairs={{0,5},{1,4},{2,7},{3,6},{4,1},{5,0},{6,3},{7,2},{8,13},{9,12},{10,... | collective-permute-start | bytes 393224 | tf_op jit(solution)/shard_map/ppermute | solution.py:290
  70.3 3.9 %collective-permute-start.5 = (bf16[2,256,128]{2,1,0:T(8,128)(2,1)S(1)}, bf16[2,256,128]{2,1,0:T(8,128)(2,1)S(1)}, u32[]{:S(2)}, u32[]{:S(2)}) collective-permute-start(bf16[2,256,128]{2,1,0:T(8,128)(2,1)S(1)} %add_tiles.14), channel_id=1, source_target_pairs={{0,5},{1,4},{2,7},{3,6},{4,1},{5,0},{6,3},{7,2},{8,13},{9,12},{10,... | collective-permute-start | bytes 393224 | tf_op jit(solution)/shard_map/ppermute | solution.py:290
  74.2 0.1 add_tiles.18
  74.3 0.1 add_tiles.19
  74.4 0.1 add_tiles.21
  74.5 4.7 %collective-permute-start.13 = (bf16[4,256,128]{2,1,0:T(8,128)(2,1)S(1)}, bf16[4,256,128]{2,1,0:T(8,128)(2,1)S(1)}, u32[]{:S(2)}, u32[]{:S(2)}) collective-permute-start(bf16[4,256,128]{2,1,0:T(8,128)(2,1)S(1)} %add_tiles.18), channel_id=1, source_target_pairs={{0,7},{1,6},{2,5},{3,4},{4,3},{5,2},{6,1},{7,0},{8,15},{9,14},{10,... | collective-permute-start | bytes 786440 | tf_op jit(solution)/shard_map/ppermute | solution.py:290
  79.3 0.1 add_tiles.22
  79.4 8.1 %collective-permute-done.3.refs_0_ = bf16[2,256,128]{2,1,0:T(8,128)(2,1)S(1)} collective-permute-done((bf16[2,256,128]{2,1,0:T(8,128)(2,1)S(1)}, bf16[2,256,128]{2,1,0:T(8,128)(2,1)S(1)}, u32[]{:S(2)}, u32[]{:S(2)}) %collective-permute-start.3) | collective-permute-done | bytes 131104 | tf_op jit(solution)/shard_map/ppermute | solution.py:290
  87.5 2.8 %collective-permute-done.5.refs_1_ = bf16[2,256,128]{2,1,0:T(8,128)(2,1)S(1)} collective-permute-done((bf16[2,256,128]{2,1,0:T(8,128)(2,1)S(1)}, bf16[2,256,128]{2,1,0:T(8,128)(2,1)S(1)}, u32[]{:S(2)}, u32[]{:S(2)}) %collective-permute-start.5) | collective-permute-done | bytes 131104 | tf_op jit(solution)/shard_map/ppermute | solution.py:290
  90.2 1.5 %collective-permute-start.22 = (bf16[4,256,128]{2,1,0:T(8,128)(2,1)S(1)}, bf16[4,256,128]{2,1,0:T(8,128)(2,1)S(1)}, u32[]{:S(2)}, u32[]{:S(2)}) collective-permute-start(bf16[4,256,128]{2,1,0:T(8,128)(2,1)S(1)} %get-tuple-element.50), channel_id=1, source_target_pairs={{0,16},{8,24},{16,0},{24,8},{1,17},{9,25},{17,1},{25,9},{2,18},{10... | collective-permute-start | bytes 786440 | tf_op jit(solution)/shard_map/ppermute | solution.py:290
  91.7 3.6 %collective-permute-start.19 = (bf16[4,256,128]{2,1,0:T(8,128)(2,1)S(1)}, bf16[4,256,128]{2,1,0:T(8,128)(2,1)S(1)}, u32[]{:S(2)}, u32[]{:S(2)}) collective-permute-start(bf16[4,256,128]{2,1,0:T(8,128)(2,1)S(1)} %add_tiles.21), channel_id=1, source_target_pairs={{0,6},{1,7},{2,4},{3,5},{4,2},{5,3},{6,0},{7,1},{8,14},{9,15},{10,... | collective-permute-start | bytes 786440 | tf_op jit(solution)/shard_map/ppermute | solution.py:290
  95.3 0.5 collective-permute-start.21
  95.8 1.1 %gather_tiles.2.refs_0_ = f32[8,256,128]{2,1,0:T(8,128)S(1)} custom-call(s32[10]{0:T(128)S(1)} %stack.40.place_ref, s32[8,4,8]{2,1,0:T(4,128)S(1)} %bitcast.16, bf16[2,256,128]{2,1,0:T(8,128)(2,1)S(1)} %collective-permute-done.3.refs_0_, bf16[2,256,128]{2,1,0:T(8,128)(2,1)S(1)} %collective-permute-done.5.refs_1_, ...), custom_call_target="tpu_custom_call" | custom-call | tf_op jit(solution)/shard_map/gather_tiles/pallas_call | solution.py:262
  96.9 0.1 add_tiles.23.refs_3_
  97.0 4.1 %collective-permute-done.19.refs_1_ = bf16[4,256,128]{2,1,0:T(8,128)(2,1)S(1)} collective-permute-done((bf16[4,256,128]{2,1,0:T(8,128)(2,1)S(1)}, bf16[4,256,128]{2,1,0:T(8,128)(2,1)S(1)}, u32[]{:S(2)}, u32[]{:S(2)}) %collective-permute-start.19) | collective-permute-done | bytes 262176 | tf_op jit(solution)/shard_map/ppermute | solution.py:290
  101.1 0.6 collective-permute-done.21.refs_2_
  101.7 2.0 %gather_tiles.3 = bf16[1024,256]{1,0:T(8,128)(2,1)} custom-call(s32[10]{0:T(128)S(1)} %stack.40.place_ref, s32[8,4,8]{2,1,0:T(4,128)S(1)} %bitcast.17, f32[8,256,128]{2,1,0:T(8,128)S(1)} %gather_tiles.2.refs_0_, bf16[4,256,128]{2,1,0:T(8,128)(2,1)S(1)} %collective-permute-done.19.refs_1_, bf16[4,256,128]{2,1,0:T(8,128)(2,1)S(1)} %collective-permute-done.21.refs_2_, ...), custom_call_target="tpu_custom_call" | custom-call | tf_op jit(solution)/shard_map/gather_tiles/pallas_call | solution.py:262
  (18 shorter events, 0.1 us)
Async XLA Ops:
  18.0 2.5 %collective-permute-start.1 = (bf16[12,256,128]{2,1,0:T(8,128)(2,1)S(1)}, bf16[12,256,128]{2,1,0:T(8,128)(2,1)S(1)}, u32[]{:S(2)}, u32[]{:S(2)}) collective-permute-start(bf16[12,256,128]{2,1,0:T(8,128)(2,1)S(1)} %get-tuple-element.30), channel_id=1, source_target_pairs={{0,8},{8,0},{16,24},{24,16},{1,9},{9,1},{17,25},{25,17},{2,10},{10... | collective-permute-start | bytes 2359304 | tf_op jit(solution)/shard_map/ppermute | solution.py:290
  24.0 2.0 %collective-permute-start.11 = (bf16[8,256,128]{2,1,0:T(8,128)(2,1)S(1)}, bf16[8,256,128]{2,1,0:T(8,128)(2,1)S(1)}, u32[]{:S(2)}, u32[]{:S(2)}) collective-permute-start(bf16[8,256,128]{2,1,0:T(8,128)(2,1)S(1)} %get-tuple-element.40), channel_id=1, source_target_pairs={{0,8},{8,0},{16,24},{24,16},{1,9},{9,1},{17,25},{25,17},{2,10},{10... | collective-permute-start | bytes 1572872 | tf_op jit(solution)/shard_map/ppermute | solution.py:290
  24.4 9.7 %collective-permute-start = (bf16[12,256,128]{2,1,0:T(8,128)(2,1)S(1)}, bf16[12,256,128]{2,1,0:T(8,128)(2,1)S(1)}, u32[]{:S(2)}, u32[]{:S(2)}) collective-permute-start(bf16[12,256,128]{2,1,0:T(8,128)(2,1)S(1)} %get-tuple-element.28), channel_id=1, source_target_pairs={{0,8},{8,0},{16,24},{24,16},{1,9},{9,1},{17,25},{25,17},{2,10},{10... | collective-permute-start | bytes 2359304 | tf_op jit(solution)/shard_map/ppermute | solution.py:290
  30.7 19.0 %collective-permute-start.17 = (bf16[12,256,128]{2,1,0:T(8,128)(2,1)S(1)}, bf16[12,256,128]{2,1,0:T(8,128)(2,1)S(1)}, u32[]{:S(2)}, u32[]{:S(2)}) collective-permute-start(bf16[12,256,128]{2,1,0:T(8,128)(2,1)S(1)} %get-tuple-element.46), channel_id=1, source_target_pairs={{0,8},{8,0},{16,24},{24,16},{1,9},{9,1},{17,25},{25,17},{2,10},{10... | collective-permute-start | bytes 2359304 | tf_op jit(solution)/shard_map/ppermute | solution.py:290
  31.1 36.6 %collective-permute-start.16 = (bf16[12,256,128]{2,1,0:T(8,128)(2,1)S(1)}, bf16[12,256,128]{2,1,0:T(8,128)(2,1)S(1)}, u32[]{:S(2)}, u32[]{:S(2)}) collective-permute-start(bf16[12,256,128]{2,1,0:T(8,128)(2,1)S(1)} %get-tuple-element.44), channel_id=1, source_target_pairs={{0,8},{8,0},{16,24},{24,16},{1,9},{9,1},{17,25},{25,17},{2,10},{10... | collective-permute-start | bytes 2359304 | tf_op jit(solution)/shard_map/ppermute | solution.py:290
  31.3 7.2 %collective-permute-start.2 = (bf16[2,256,128]{2,1,0:T(8,128)(2,1)S(1)}, bf16[2,256,128]{2,1,0:T(8,128)(2,1)S(1)}, u32[]{:S(2)}, u32[]{:S(2)}) collective-permute-start(bf16[2,256,128]{2,1,0:T(8,128)(2,1)S(1)} %get-tuple-element.32.refs_0_), channel_id=1, source_target_pairs={{0,16},{8,24},{16,0},{24,8},{1,17},{9,25},{17,1},{25,9},{2,18},{10... | collective-permute-start | bytes 393224 | tf_op jit(solution)/shard_map/ppermute | solution.py:290
  34.1 21.2 %collective-permute-start.10 = (bf16[8,256,128]{2,1,0:T(8,128)(2,1)S(1)}, bf16[8,256,128]{2,1,0:T(8,128)(2,1)S(1)}, u32[]{:S(2)}, u32[]{:S(2)}) collective-permute-start(bf16[8,256,128]{2,1,0:T(8,128)(2,1)S(1)} %get-tuple-element.38), channel_id=1, source_target_pairs={{0,8},{8,0},{16,24},{24,16},{1,9},{9,1},{17,25},{25,17},{2,10},{10... | collective-permute-start | bytes 1572872 | tf_op jit(solution)/shard_map/ppermute | solution.py:290
  34.1 7.2 %collective-permute-start.4 = (bf16[2,256,128]{2,1,0:T(8,128)(2,1)S(1)}, bf16[2,256,128]{2,1,0:T(8,128)(2,1)S(1)}, u32[]{:S(2)}, u32[]{:S(2)}) collective-permute-start(bf16[2,256,128]{2,1,0:T(8,128)(2,1)S(1)} %get-tuple-element.33), channel_id=1, source_target_pairs={{0,16},{8,24},{16,0},{24,8},{1,17},{9,25},{17,1},{25,9},{2,18},{10... | collective-permute-start | bytes 393224 | tf_op jit(solution)/shard_map/ppermute | solution.py:290
  38.5 9.2 %collective-permute-start.6 = (bf16[4,256,128]{2,1,0:T(8,128)(2,1)S(1)}, bf16[4,256,128]{2,1,0:T(8,128)(2,1)S(1)}, u32[]{:S(2)}, u32[]{:S(2)}) collective-permute-start(bf16[4,256,128]{2,1,0:T(8,128)(2,1)S(1)} %get-tuple-element.34), channel_id=1, source_target_pairs={{0,16},{8,24},{16,0},{24,8},{1,17},{9,25},{17,1},{25,9},{2,18},{10... | collective-permute-start | bytes 786440 | tf_op jit(solution)/shard_map/ppermute | solution.py:290
  41.3 12.0 %collective-permute-start.8 = (bf16[4,256,128]{2,1,0:T(8,128)(2,1)S(1)}, bf16[4,256,128]{2,1,0:T(8,128)(2,1)S(1)}, u32[]{:S(2)}, u32[]{:S(2)}) collective-permute-start(bf16[4,256,128]{2,1,0:T(8,128)(2,1)S(1)} %get-tuple-element.35), channel_id=1, source_target_pairs={{0,16},{8,24},{16,0},{24,8},{1,17},{9,25},{17,1},{25,9},{2,18},{10... | collective-permute-start | bytes 786440 | tf_op jit(solution)/shard_map/ppermute | solution.py:290
  47.7 11.2 %collective-permute-start.12 = (bf16[4,256,128]{2,1,0:T(8,128)(2,1)S(1)}, bf16[4,256,128]{2,1,0:T(8,128)(2,1)S(1)}, u32[]{:S(2)}, u32[]{:S(2)}) collective-permute-start(bf16[4,256,128]{2,1,0:T(8,128)(2,1)S(1)} %get-tuple-element.42.refs_0_), channel_id=1, source_target_pairs={{0,16},{8,24},{16,0},{24,8},{1,17},{9,25},{17,1},{25,9},{2,18},{10... | collective-permute-start | bytes 786440 | tf_op jit(solution)/shard_map/ppermute | solution.py:290
  49.7 14.8 %collective-permute-start.14 = (bf16[4,256,128]{2,1,0:T(8,128)(2,1)S(1)}, bf16[4,256,128]{2,1,0:T(8,128)(2,1)S(1)}, u32[]{:S(2)}, u32[]{:S(2)}) collective-permute-start(bf16[4,256,128]{2,1,0:T(8,128)(2,1)S(1)} %get-tuple-element.43), channel_id=1, source_target_pairs={{0,16},{8,24},{16,0},{24,8},{1,17},{9,25},{17,1},{25,9},{2,18},{10... | collective-permute-start | bytes 786440 | tf_op jit(solution)/shard_map/ppermute | solution.py:290
  53.3 17.0 %collective-permute-start.18 = (bf16[4,256,128]{2,1,0:T(8,128)(2,1)S(1)}, bf16[4,256,128]{2,1,0:T(8,128)(2,1)S(1)}, u32[]{:S(2)}, u32[]{:S(2)}) collective-permute-start(bf16[4,256,128]{2,1,0:T(8,128)(2,1)S(1)} %get-tuple-element.48), channel_id=1, source_target_pairs={{0,16},{8,24},{16,0},{24,8},{1,17},{9,25},{17,1},{25,9},{2,18},{10... | collective-permute-start | bytes 786440 | tf_op jit(solution)/shard_map/ppermute | solution.py:290
  55.3 19.2 %collective-permute-start.20 = (bf16[4,256,128]{2,1,0:T(8,128)(2,1)S(1)}, bf16[4,256,128]{2,1,0:T(8,128)(2,1)S(1)}, u32[]{:S(2)}, u32[]{:S(2)}) collective-permute-start(bf16[4,256,128]{2,1,0:T(8,128)(2,1)S(1)} %get-tuple-element.49), channel_id=1, source_target_pairs={{0,16},{8,24},{16,0},{24,8},{1,17},{9,25},{17,1},{25,9},{2,18},{10... | collective-permute-start | bytes 786440 | tf_op jit(solution)/shard_map/ppermute | solution.py:290
  58.9 32.8 %collective-permute-start.7 = (bf16[4,256,128]{2,1,0:T(8,128)(2,1)S(1)}, bf16[4,256,128]{2,1,0:T(8,128)(2,1)S(1)}, u32[]{:S(2)}, u32[]{:S(2)}) collective-permute-start(bf16[4,256,128]{2,1,0:T(8,128)(2,1)S(1)} %add_tiles.15), channel_id=1, source_target_pairs={{0,4},{1,5},{2,6},{3,7},{4,0},{5,1},{6,2},{7,3},{8,12},{9,13},{10,... | collective-permute-start | bytes 786440 | tf_op jit(solution)/shard_map/ppermute | solution.py:290
  64.5 30.8 %collective-permute-start.9 = (bf16[4,256,128]{2,1,0:T(8,128)(2,1)S(1)}, bf16[4,256,128]{2,1,0:T(8,128)(2,1)S(1)}, u32[]{:S(2)}, u32[]{:S(2)}) collective-permute-start(bf16[4,256,128]{2,1,0:T(8,128)(2,1)S(1)} %add_tiles.16), channel_id=1, source_target_pairs={{0,3},{1,2},{2,1},{3,0},{4,7},{5,6},{6,5},{7,4},{8,11},{9,10},{10,... | collective-permute-start | bytes 786440 | tf_op jit(solution)/shard_map/ppermute | solution.py:290
  67.7 19.8 %collective-permute-start.3 = (bf16[2,256,128]{2,1,0:T(8,128)(2,1)S(1)}, bf16[2,256,128]{2,1,0:T(8,128)(2,1)S(1)}, u32[]{:S(2)}, u32[]{:S(2)}) collective-permute-start(bf16[2,256,128]{2,1,0:T(8,128)(2,1)S(1)} %add_tiles.13), channel_id=1, source_target_pairs={{0,5},{1,4},{2,7},{3,6},{4,1},{5,0},{6,3},{7,2},{8,13},{9,12},{10,... | collective-permute-start | bytes 393224 | tf_op jit(solution)/shard_map/ppermute | solution.py:290
  70.3 19.9 %collective-permute-start.5 = (bf16[2,256,128]{2,1,0:T(8,128)(2,1)S(1)}, bf16[2,256,128]{2,1,0:T(8,128)(2,1)S(1)}, u32[]{:S(2)}, u32[]{:S(2)}) collective-permute-start(bf16[2,256,128]{2,1,0:T(8,128)(2,1)S(1)} %add_tiles.14), channel_id=1, source_target_pairs={{0,5},{1,4},{2,7},{3,6},{4,1},{5,0},{6,3},{7,2},{8,13},{9,12},{10,... | collective-permute-start | bytes 393224 | tf_op jit(solution)/shard_map/ppermute | solution.py:290
  74.4 21.3 %copy-start = (s32[8,8,4]{1,2,0:T(4,128)S(1)}, s32[8,8,4]{1,2,0:T(4,128)}, u32[]{:S(2)}) copy-start(s32[8,8,4]{1,2,0:T(4,128)} %param.9) | copy-start | bytes 3076
  74.5 21.2 %collective-permute-start.13 = (bf16[4,256,128]{2,1,0:T(8,128)(2,1)S(1)}, bf16[4,256,128]{2,1,0:T(8,128)(2,1)S(1)}, u32[]{:S(2)}, u32[]{:S(2)}) collective-permute-start(bf16[4,256,128]{2,1,0:T(8,128)(2,1)S(1)} %add_tiles.18), channel_id=1, source_target_pairs={{0,7},{1,6},{2,5},{3,4},{4,3},{5,2},{6,1},{7,0},{8,15},{9,14},{10,... | collective-permute-start | bytes 786440 | tf_op jit(solution)/shard_map/ppermute | solution.py:290
  87.5 8.3 %collective-permute-start.15 = (bf16[4,256,128]{2,1,0:T(8,128)(2,1)S(1)}, bf16[4,256,128]{2,1,0:T(8,128)(2,1)S(1)}, u32[]{:S(2)}, u32[]{:S(2)}) collective-permute-start(bf16[4,256,128]{2,1,0:T(8,128)(2,1)S(1)} %add_tiles.19), channel_id=1, source_target_pairs={{0,2},{1,3},{2,0},{3,1},{4,6},{5,7},{6,4},{7,5},{8,10},{9,11},{10,... | collective-permute-start | bytes 786440 | tf_op jit(solution)/shard_map/ppermute | solution.py:290
  90.2 6.7 %collective-permute-start.22 = (bf16[4,256,128]{2,1,0:T(8,128)(2,1)S(1)}, bf16[4,256,128]{2,1,0:T(8,128)(2,1)S(1)}, u32[]{:S(2)}, u32[]{:S(2)}) collective-permute-start(bf16[4,256,128]{2,1,0:T(8,128)(2,1)S(1)} %get-tuple-element.50), channel_id=1, source_target_pairs={{0,16},{8,24},{16,0},{24,8},{1,17},{9,25},{17,1},{25,9},{2,18},{10... | collective-permute-start | bytes 786440 | tf_op jit(solution)/shard_map/ppermute | solution.py:290
  91.7 9.4 %collective-permute-start.19 = (bf16[4,256,128]{2,1,0:T(8,128)(2,1)S(1)}, bf16[4,256,128]{2,1,0:T(8,128)(2,1)S(1)}, u32[]{:S(2)}, u32[]{:S(2)}) collective-permute-start(bf16[4,256,128]{2,1,0:T(8,128)(2,1)S(1)} %add_tiles.21), channel_id=1, source_target_pairs={{0,6},{1,7},{2,4},{3,5},{4,2},{5,3},{6,0},{7,1},{8,14},{9,15},{10,... | collective-permute-start | bytes 786440 | tf_op jit(solution)/shard_map/ppermute | solution.py:290
  95.3 6.4 %collective-permute-start.21 = (bf16[4,256,128]{2,1,0:T(8,128)(2,1)S(1)}, bf16[4,256,128]{2,1,0:T(8,128)(2,1)S(1)}, u32[]{:S(2)}, u32[]{:S(2)}) collective-permute-start(bf16[4,256,128]{2,1,0:T(8,128)(2,1)S(1)} %add_tiles.22), channel_id=1, source_target_pairs={{0,1},{1,0},{2,3},{3,2},{4,5},{5,4},{6,7},{7,6},{8,9},{9,8},{10,11... | collective-permute-start | bytes 786440 | tf_op jit(solution)/shard_map/ppermute | solution.py:290
where the time goes:
time: 106 us; the launch traced here: 104 us
  waiting for transfers between devices  37.4 us (35%)
  starting transfers between devices  35.8 us (34%)
  Pallas kernels  30.3 us (29%)
    ppermute x23, waiting for transfers between devices, swap(): lax.ppermute(array, axis, [(i, i ^ bit) for i in range(lax.axis_size(axis...  37.4 us
    ppermute x23, starting transfers between devices, swap(): lax.ppermute(array, axis, [(i, i ^ bit) for i in range(lax.axis_size(axis...  35.8 us
    pallas_call x1, Pallas kernels, first_products(): pl.pallas_call(functools.partial(first_kernel, groups=groups), grid_spec=...  17.9 us
    pallas_call x2, Pallas kernels, rest_products(): pl.pallas_call(functools.partial(rest_kernel, count=replicas), grid_spec=...  7.87 us
    pallas_call x2, Pallas kernels, gather_tiles(): pl.pallas_call(functools.partial(gather_kernel, plan=tuple(((distance, at...  3.16 us
  transfers between devices with their start and end apart: 23, of which 12 were waited for; matrix products, arithmetic and copies ran while one was open for 0% of the time, Pallas kernels for 7%

commit v1 on v0

--- a/solution.py
+++ b/solution.py
@@ -55,8 +55,9 @@
 
 def distances(groups):
     half = groups // 2
-    far, near = [n ^ 1 for n in range(half, groups)], list(range(half - 1, -1, -1))
-    return far[:2] + near[:1] + far[2:3] + near[1:2] + far[3:] + near[2:]
+    far, near = list(range(half, groups)), list(range(half - 1, -1, -1))
+    far = far[1:2] + far[:1] + far[2:]
+    return far[:3] + [n for n in near if n & 1] + far[3:] + [n for n in near if not n & 1]
 
 
 def put_products(flip, coef, out_refs):

time: 106 us -> 113 us (1.066); the launches traced: 104 us -> 112 us
  waiting for transfers between devices: 37.4 us -> 48.9 us
  starting transfers between devices: 35.8 us -> 33 us
    ppermute x23, waiting for transfers between devices: 37.4 us -> 48.9 us  [swap(): lax.ppermute(array, axis, [(i, i ^ bit) for i in range(lax.axis_size(axis...]
    ppermute x23, starting transfers between devices: 35.8 us -> 33 us  [swap(): lax.ppermute(array, axis, [(i, i ^ bit) for i in range(lax.axis_size(axis...]
  transfers between devices with their start and end apart: 23 -> 23, of which waited for: 12 -> 14; matrix products, arithmetic and copies ran while one was open for 0% -> 0% of each run, Pallas kernels for 7% -> 6%
where the time goes in v1:
time: 113 us; the launch traced here: 112 us
  waiting for transfers between devices  48.9 us (43%)
  starting transfers between devices  33 us (29%)
  Pallas kernels  30.3 us (27%)
    ppermute x23, waiting for transfers between devices, swap(): lax.ppermute(array, axis, [(i, i ^ bit) for i in range(lax.axis_size(axis...  48.9 us
    ppermute x23, starting transfers between devices, swap(): lax.ppermute(array, axis, [(i, i ^ bit) for i in range(lax.axis_size(axis...  33 us
    pallas_call x1, Pallas kernels, first_products(): pl.pallas_call(functools.partial(first_kernel, groups=groups), grid_spec=...  17.9 us
    pallas_call x2, Pallas kernels, rest_products(): pl.pallas_call(functools.partial(rest_kernel, count=replicas), grid_spec=...  7.87 us
    pallas_call x2, Pallas kernels, gather_tiles(): pl.pallas_call(functools.partial(gather_kernel, plan=tuple(((distance, at...  3.16 us
  transfers between devices with their start and end apart: 23, of which 14 were waited for; matrix products, arithmetic and copies ran while one was open for 0% of the time, Pallas kernels for 6%

profile of v1, /device:TPU:0, one launch (start us, length us, event | category | flops | bytes accessed | tf_op | source)
XLA Modules:
  0.0 112.4 jit_solution(8204336518119682148)
XLA Ops:
  0.1 17.9 %first_products.1 = (bf16[1024,4096]{1,0:T(8,128)(2,1)S(1)}, bf16[1024,1024]{1,0:T(8,128)(2,1)S(1)}, bf16[12,256,128]{2,1,0:T(8,128)(2,1)S(1)}, bf16[12,256,128]...) custom-call(s32[10]{0:T(128)S(1)} %stack.40.place_ref, f32[8]{0:T(128)} %scale_ref.1, ...), custom_call_target="tpu_custom_call" | custom-call | flops 8589934592 | bytes 16777216 | tf_op jit(solution)/shard_map/first_products/pallas_call | solution.py:130
  18.0 0.6 collective-permute-start.1
  18.6 1.9 %collective-permute-done.1.refs_0_ = bf16[12,256,128]{2,1,0:T(8,128)(2,1)S(1)} collective-permute-done((bf16[12,256,128]{2,1,0:T(8,128)(2,1)S(1)}, bf16[12,256,128]{2,1,0:T(8,128)(2,1)S(1)}, u32[]{:S(2)}, u32[]{:S(2)}) %collective-permute-start.1) | collective-permute-done | bytes 786464 | tf_op jit(solution)/shard_map/ppermute | solution.py:291
  20.5 0.2 add_tiles.12
  20.7 3.3 %rest_products.2 = (bf16[8,256,128]{2,1,0:T(8,128)(2,1)S(1)}, bf16[8,256,128]{2,1,0:T(8,128)(2,1)S(1)}, bf16[8,256,128]{2,1,0:T(8,128)(2,1)S(1)}, bf16[8,256,128]{2,1,0:T(8,128)(2,1)S(1)}) custom-call(s32[10]{0:T(128)S(1)} %stack.40.place_ref, bf16[1024,4096]{1,0:T(8,128)(2,1)S(1)} %get-tuple-element.36.coef_ref, ...), custom_call_target="tpu_custom_call" | custom-call | flops 2147483648 | bytes 6291456 | tf_op jit(solution)/shard_map/rest_products/pallas_call | solution.py:178
  24.0 0.4 collective-permute-start.11
  24.4 0.1 collective-permute-start
  24.5 1.4 %collective-permute-done.11.refs_0_ = bf16[8,256,128]{2,1,0:T(8,128)(2,1)S(1)} collective-permute-done((bf16[8,256,128]{2,1,0:T(8,128)(2,1)S(1)}, bf16[8,256,128]{2,1,0:T(8,128)(2,1)S(1)}, u32[]{:S(2)}, u32[]{:S(2)}) %collective-permute-start.11) | collective-permute-done | bytes 524320 | tf_op jit(solution)/shard_map/ppermute | solution.py:291
  25.9 0.1 add_tiles.17
  26.1 4.6 %rest_products.3 = (bf16[12,256,128]{2,1,0:T(8,128)(2,1)S(1)}, bf16[12,256,128]{2,1,0:T(8,128)(2,1)S(1)}, bf16[12,256,128]{2,1,0:T(8,128)(2,1)S(1)}, bf16[12,256,128]{2,1,0:T(8,128)(2,1)S(1)}) custom-call(s32[10]{0:T(128)S(1)} %stack.40.place_ref, bf16[1024,4096]{1,0:T(8,128)(2,1)S(1)} %get-tuple-element.36.coef_ref, ...), custom_call_target="tpu_custom_call" | custom-call | flops 3221225472 | bytes 8388608 | tf_op jit(solution)/shard_map/rest_products/pallas_call | solution.py:178
  30.7 0.4 collective-permute-start.17
  31.1 0.1 collective-permute-start.16
  31.3 2.9 %collective-permute-start.2 = (bf16[2,256,128]{2,1,0:T(8,128)(2,1)S(1)}, bf16[2,256,128]{2,1,0:T(8,128)(2,1)S(1)}, u32[]{:S(2)}, u32[]{:S(2)}) collective-permute-start(bf16[2,256,128]{2,1,0:T(8,128)(2,1)S(1)} %get-tuple-element.32.refs_0_), channel_id=1, source_target_pairs={{0,16},{8,24},{16,0},{24,8},{1,17},{9,25},{17,1},{25,9},{2,18},{10... | collective-permute-start | bytes 393224 | tf_op jit(solution)/shard_map/ppermute | solution.py:291
  34.1 0.1 collective-permute-start.4
  34.3 4.2 %collective-permute-done.2.refs_2_ = bf16[2,256,128]{2,1,0:T(8,128)(2,1)S(1)} collective-permute-done((bf16[2,256,128]{2,1,0:T(8,128)(2,1)S(1)}, bf16[2,256,128]{2,1,0:T(8,128)(2,1)S(1)}, u32[]{:S(2)}, u32[]{:S(2)}) %collective-permute-start.2) | collective-permute-done | bytes 131104 | tf_op jit(solution)/shard_map/ppermute | solution.py:291
  38.5 2.0 %collective-permute-start.6 = (bf16[4,256,128]{2,1,0:T(8,128)(2,1)S(1)}, bf16[4,256,128]{2,1,0:T(8,128)(2,1)S(1)}, u32[]{:S(2)}, u32[]{:S(2)}) collective-permute-start(bf16[4,256,128]{2,1,0:T(8,128)(2,1)S(1)} %get-tuple-element.34), channel_id=1, source_target_pairs={{0,16},{8,24},{16,0},{24,8},{1,17},{9,25},{17,1},{25,9},{2,18},{10... | collective-permute-start | bytes 786440 | tf_op jit(solution)/shard_map/ppermute | solution.py:291
  40.5 0.8 collective-permute-done.4.refs_2_
  41.3 2.0 %collective-permute-start.8 = (bf16[4,256,128]{2,1,0:T(8,128)(2,1)S(1)}, bf16[4,256,128]{2,1,0:T(8,128)(2,1)S(1)}, u32[]{:S(2)}, u32[]{:S(2)}) collective-permute-start(bf16[4,256,128]{2,1,0:T(8,128)(2,1)S(1)} %get-tuple-element.35), channel_id=1, source_target_pairs={{0,16},{8,24},{16,0},{24,8},{1,17},{9,25},{17,1},{25,9},{2,18},{10... | collective-permute-start | bytes 786440 | tf_op jit(solution)/shard_map/ppermute | solution.py:291
  43.3 4.3 %collective-permute-done.6.refs_2_ = bf16[4,256,128]{2,1,0:T(8,128)(2,1)S(1)} collective-permute-done((bf16[4,256,128]{2,1,0:T(8,128)(2,1)S(1)}, bf16[4,256,128]{2,1,0:T(8,128)(2,1)S(1)}, u32[]{:S(2)}, u32[]{:S(2)}) %collective-permute-start.6) | collective-permute-done | bytes 262176 | tf_op jit(solution)/shard_map/ppermute | solution.py:291
  47.7 2.0 %collective-permute-start.12 = (bf16[4,256,128]{2,1,0:T(8,128)(2,1)S(1)}, bf16[4,256,128]{2,1,0:T(8,128)(2,1)S(1)}, u32[]{:S(2)}, u32[]{:S(2)}) collective-permute-start(bf16[4,256,128]{2,1,0:T(8,128)(2,1)S(1)} %get-tuple-element.42.refs_0_), channel_id=1, source_target_pairs={{0,16},{8,24},{16,0},{24,8},{1,17},{9,25},{17,1},{25,9},{2,18},{10... | collective-permute-start | bytes 786440 | tf_op jit(solution)/shard_map/ppermute | solution.py:291
  49.7 0.2 add_tiles.20
  49.9 3.4 %collective-permute-done.8.refs_2_ = bf16[4,256,128]{2,1,0:T(8,128)(2,1)S(1)} collective-permute-done((bf16[4,256,128]{2,1,0:T(8,128)(2,1)S(1)}, bf16[4,256,128]{2,1,0:T(8,128)(2,1)S(1)}, u32[]{:S(2)}, u32[]{:S(2)}) %collective-permute-start.8) | collective-permute-done | bytes 262176 | tf_op jit(solution)/shard_map/ppermute | solution.py:291
  53.3 2.0 %collective-permute-start.18 = (bf16[4,256,128]{2,1,0:T(8,128)(2,1)S(1)}, bf16[4,256,128]{2,1,0:T(8,128)(2,1)S(1)}, u32[]{:S(2)}, u32[]{:S(2)}) collective-permute-start(bf16[4,256,128]{2,1,0:T(8,128)(2,1)S(1)} %get-tuple-element.48), channel_id=1, source_target_pairs={{0,16},{8,24},{16,0},{24,8},{1,17},{9,25},{17,1},{25,9},{2,18},{10... | collective-permute-start | bytes 786440 | tf_op jit(solution)/shard_map/ppermute | solution.py:291
  55.3 0.1 add_tiles.15
  55.4 0.1 add_tiles.16
  55.5 3.4 %collective-permute-done.12.refs_2_ = bf16[4,256,128]{2,1,0:T(8,128)(2,1)S(1)} collective-permute-done((bf16[4,256,128]{2,1,0:T(8,128)(2,1)S(1)}, bf16[4,256,128]{2,1,0:T(8,128)(2,1)S(1)}, u32[]{:S(2)}, u32[]{:S(2)}) %collective-permute-start.12) | collective-permute-done | bytes 262176 | tf_op jit(solution)/shard_map/ppermute | solution.py:291
  58.9 3.1 %collective-permute-start.7 = (bf16[4,256,128]{2,1,0:T(8,128)(2,1)S(1)}, bf16[4,256,128]{2,1,0:T(8,128)(2,1)S(1)}, u32[]{:S(2)}, u32[]{:S(2)}) collective-permute-start(bf16[4,256,128]{2,1,0:T(8,128)(2,1)S(1)} %add_tiles.15), channel_id=1, source_target_pairs={{0,4},{1,5},{2,6},{3,7},{4,0},{5,1},{6,2},{7,3},{8,12},{9,13},{10,... | collective-permute-start | bytes 786440 | tf_op jit(solution)/shard_map/ppermute | solution.py:291
  62.0 2.5 %collective-permute-done.14.refs_2_ = bf16[4,256,128]{2,1,0:T(8,128)(2,1)S(1)} collective-permute-done((bf16[4,256,128]{2,1,0:T(8,128)(2,1)S(1)}, bf16[4,256,128]{2,1,0:T(8,128)(2,1)S(1)}, u32[]{:S(2)}, u32[]{:S(2)}) %collective-permute-start.14) | collective-permute-done | bytes 262176 | tf_op jit(solution)/shard_map/ppermute | solution.py:291
  64.5 4.1 %collective-permute-start.9 = (bf16[4,256,128]{2,1,0:T(8,128)(2,1)S(1)}, bf16[4,256,128]{2,1,0:T(8,128)(2,1)S(1)}, u32[]{:S(2)}, u32[]{:S(2)}) collective-permute-start(bf16[4,256,128]{2,1,0:T(8,128)(2,1)S(1)} %add_tiles.16), channel_id=1, source_target_pairs={{0,6},{1,7},{2,4},{3,5},{4,2},{5,3},{6,0},{7,1},{8,14},{9,15},{10,... | collective-permute-start | bytes 786440 | tf_op jit(solution)/shard_map/ppermute | solution.py:291
  68.8 0.5 collective-permute-start.3
  69.2 0.9 collective-permute-done.18.refs_2_
  70.1 4.1 %collective-permute-start.5 = (bf16[2,256,128]{2,1,0:T(8,128)(2,1)S(1)}, bf16[2,256,128]{2,1,0:T(8,128)(2,1)S(1)}, u32[]{:S(2)}, u32[]{:S(2)}) collective-permute-start(bf16[2,256,128]{2,1,0:T(8,128)(2,1)S(1)} %add_tiles.14), channel_id=1, source_target_pairs={{0,5},{1,4},{2,7},{3,6},{4,1},{5,0},{6,3},{7,2},{8,13},{9,12},{10,... | collective-permute-start | bytes 393224 | tf_op jit(solution)/shard_map/ppermute | solution.py:291
  74.2 0.1 add_tiles.18
  74.3 0.1 add_tiles.19
  74.4 0.1 add_tiles.21
  74.6 2.7 %collective-permute-start.13 = (bf16[4,256,128]{2,1,0:T(8,128)(2,1)S(1)}, bf16[4,256,128]{2,1,0:T(8,128)(2,1)S(1)}, u32[]{:S(2)}, u32[]{:S(2)}) collective-permute-start(bf16[4,256,128]{2,1,0:T(8,128)(2,1)S(1)} %add_tiles.18), channel_id=1, source_target_pairs={{0,3},{1,2},{2,1},{3,0},{4,7},{5,6},{6,5},{7,4},{8,11},{9,10},{10,... | collective-permute-start | bytes 786440 | tf_op jit(solution)/shard_map/ppermute | solution.py:291
  77.2 0.1 add_tiles.22
  77.3 15.6 %collective-permute-done.3.refs_0_ = bf16[2,256,128]{2,1,0:T(8,128)(2,1)S(1)} collective-permute-done((bf16[2,256,128]{2,1,0:T(8,128)(2,1)S(1)}, bf16[2,256,128]{2,1,0:T(8,128)(2,1)S(1)}, u32[]{:S(2)}, u32[]{:S(2)}) %collective-permute-start.3) | collective-permute-done | bytes 131104 | tf_op jit(solution)/shard_map/ppermute | solution.py:291
  92.9 0.4 collective-permute-start.15
  93.4 1.3 %collective-permute-done.5.refs_1_ = bf16[2,256,128]{2,1,0:T(8,128)(2,1)S(1)} collective-permute-done((bf16[2,256,128]{2,1,0:T(8,128)(2,1)S(1)}, bf16[2,256,128]{2,1,0:T(8,128)(2,1)S(1)}, u32[]{:S(2)}, u32[]{:S(2)}) %collective-permute-start.5) | collective-permute-done | bytes 131104 | tf_op jit(solution)/shard_map/ppermute | solution.py:291
  94.6 1.5 %collective-permute-start.22 = (bf16[4,256,128]{2,1,0:T(8,128)(2,1)S(1)}, bf16[4,256,128]{2,1,0:T(8,128)(2,1)S(1)}, u32[]{:S(2)}, u32[]{:S(2)}) collective-permute-start(bf16[4,256,128]{2,1,0:T(8,128)(2,1)S(1)} %get-tuple-element.50), channel_id=1, source_target_pairs={{0,16},{8,24},{16,0},{24,8},{1,17},{9,25},{17,1},{25,9},{2,18},{10... | collective-permute-start | bytes 786440 | tf_op jit(solution)/shard_map/ppermute | solution.py:291
  96.1 3.7 %collective-permute-start.19 = (bf16[4,256,128]{2,1,0:T(8,128)(2,1)S(1)}, bf16[4,256,128]{2,1,0:T(8,128)(2,1)S(1)}, u32[]{:S(2)}, u32[]{:S(2)}) collective-permute-start(bf16[4,256,128]{2,1,0:T(8,128)(2,1)S(1)} %add_tiles.21), channel_id=1, source_target_pairs={{0,7},{1,6},{2,5},{3,4},{4,3},{5,2},{6,1},{7,0},{8,15},{9,14},{10,... | collective-permute-start | bytes 786440 | tf_op jit(solution)/shard_map/ppermute | solution.py:291
  99.9 3.7 %collective-permute-done.15.refs_5_ = bf16[4,256,128]{2,1,0:T(8,128)(2,1)S(1)} collective-permute-done((bf16[4,256,128]{2,1,0:T(8,128)(2,1)S(1)}, bf16[4,256,128]{2,1,0:T(8,128)(2,1)S(1)}, u32[]{:S(2)}, u32[]{:S(2)}) %collective-permute-start.15) | collective-permute-done | bytes 262176 | tf_op jit(solution)/shard_map/ppermute | solution.py:291
  103.5 1.1 %gather_tiles.2.refs_0_ = f32[8,256,128]{2,1,0:T(8,128)S(1)} custom-call(s32[10]{0:T(128)S(1)} %stack.40.place_ref, s32[8,4,8]{2,1,0:T(4,128)S(1)} %bitcast.16, bf16[2,256,128]{2,1,0:T(8,128)(2,1)S(1)} %collective-permute-done.3.refs_0_, bf16[2,256,128]{2,1,0:T(8,128)(2,1)S(1)} %collective-permute-done.5.refs_1_, ...), custom_call_target="tpu_custom_call" | custom-call | tf_op jit(solution)/shard_map/gather_tiles/pallas_call | solution.py:263
  104.7 0.1 add_tiles.23.refs_3_
  104.8 3.2 %collective-permute-done.19.refs_1_ = bf16[4,256,128]{2,1,0:T(8,128)(2,1)S(1)} collective-permute-done((bf16[4,256,128]{2,1,0:T(8,128)(2,1)S(1)}, bf16[4,256,128]{2,1,0:T(8,128)(2,1)S(1)}, u32[]{:S(2)}, u32[]{:S(2)}) %collective-permute-start.19) | collective-permute-done | bytes 262176 | tf_op jit(solution)/shard_map/ppermute | solution.py:291
  108.0 2.4 %collective-permute-done.21.refs_2_ = bf16[4,256,128]{2,1,0:T(8,128)(2,1)S(1)} collective-permute-done((bf16[4,256,128]{2,1,0:T(8,128)(2,1)S(1)}, bf16[4,256,128]{2,1,0:T(8,128)(2,1)S(1)}, u32[]{:S(2)}, u32[]{:S(2)}) %collective-permute-start.21) | collective-permute-done | bytes 262176 | tf_op jit(solution)/shard_map/ppermute | solution.py:291
  110.4 2.0 %gather_tiles.3 = bf16[1024,256]{1,0:T(8,128)(2,1)} custom-call(s32[10]{0:T(128)S(1)} %stack.40.place_ref, s32[8,4,8]{2,1,0:T(4,128)S(1)} %bitcast.17, f32[8,256,128]{2,1,0:T(8,128)S(1)} %gather_tiles.2.refs_0_, bf16[4,256,128]{2,1,0:T(8,128)(2,1)S(1)} %collective-permute-done.19.refs_1_, bf16[4,256,128]{2,1,0:T(8,128)(2,1)S(1)} %collective-permute-done.21.refs_2_, ...), custom_call_target="tpu_custom_call" | custom-call | tf_op jit(solution)/shard_map/gather_tiles/pallas_call | solution.py:263
  (18 shorter events, 0.3 us)
Async XLA Ops:
  18.0 2.5 %collective-permute-start.1 = (bf16[12,256,128]{2,1,0:T(8,128)(2,1)S(1)}, bf16[12,256,128]{2,1,0:T(8,128)(2,1)S(1)}, u32[]{:S(2)}, u32[]{:S(2)}) collective-permute-start(bf16[12,256,128]{2,1,0:T(8,128)(2,1)S(1)} %get-tuple-element.30), channel_id=1, source_target_pairs={{0,8},{8,0},{16,24},{24,16},{1,9},{9,1},{17,25},{25,17},{2,10},{10... | collective-permute-start | bytes 2359304 | tf_op jit(solution)/shard_map/ppermute | solution.py:291
  24.0 2.0 %collective-permute-start.11 = (bf16[8,256,128]{2,1,0:T(8,128)(2,1)S(1)}, bf16[8,256,128]{2,1,0:T(8,128)(2,1)S(1)}, u32[]{:S(2)}, u32[]{:S(2)}) collective-permute-start(bf16[8,256,128]{2,1,0:T(8,128)(2,1)S(1)} %get-tuple-element.40), channel_id=1, source_target_pairs={{0,8},{8,0},{16,24},{24,16},{1,9},{9,1},{17,25},{25,17},{2,10},{10... | collective-permute-start | bytes 1572872 | tf_op jit(solution)/shard_map/ppermute | solution.py:291
  24.4 9.7 %collective-permute-start = (bf16[12,256,128]{2,1,0:T(8,128)(2,1)S(1)}, bf16[12,256,128]{2,1,0:T(8,128)(2,1)S(1)}, u32[]{:S(2)}, u32[]{:S(2)}) collective-permute-start(bf16[12,256,128]{2,1,0:T(8,128)(2,1)S(1)} %get-tuple-element.28), channel_id=1, source_target_pairs={{0,8},{8,0},{16,24},{24,16},{1,9},{9,1},{17,25},{25,17},{2,10},{10... | collective-permute-start | bytes 2359304 | tf_op jit(solution)/shard_map/ppermute | solution.py:291
  30.7 19.0 %collective-permute-start.17 = (bf16[12,256,128]{2,1,0:T(8,128)(2,1)S(1)}, bf16[12,256,128]{2,1,0:T(8,128)(2,1)S(1)}, u32[]{:S(2)}, u32[]{:S(2)}) collective-permute-start(bf16[12,256,128]{2,1,0:T(8,128)(2,1)S(1)} %get-tuple-element.46), channel_id=1, source_target_pairs={{0,8},{8,0},{16,24},{24,16},{1,9},{9,1},{17,25},{25,17},{2,10},{10... | collective-permute-start | bytes 2359304 | tf_op jit(solution)/shard_map/ppermute | solution.py:291
  31.1 37.6 %collective-permute-start.16 = (bf16[12,256,128]{2,1,0:T(8,128)(2,1)S(1)}, bf16[12,256,128]{2,1,0:T(8,128)(2,1)S(1)}, u32[]{:S(2)}, u32[]{:S(2)}) collective-permute-start(bf16[12,256,128]{2,1,0:T(8,128)(2,1)S(1)} %get-tuple-element.44), channel_id=1, source_target_pairs={{0,8},{8,0},{16,24},{24,16},{1,9},{9,1},{17,25},{25,17},{2,10},{10... | collective-permute-start | bytes 2359304 | tf_op jit(solution)/shard_map/ppermute | solution.py:291
  31.3 7.2 %collective-permute-start.2 = (bf16[2,256,128]{2,1,0:T(8,128)(2,1)S(1)}, bf16[2,256,128]{2,1,0:T(8,128)(2,1)S(1)}, u32[]{:S(2)}, u32[]{:S(2)}) collective-permute-start(bf16[2,256,128]{2,1,0:T(8,128)(2,1)S(1)} %get-tuple-element.32.refs_0_), channel_id=1, source_target_pairs={{0,16},{8,24},{16,0},{24,8},{1,17},{9,25},{17,1},{25,9},{2,18},{10... | collective-permute-start | bytes 393224 | tf_op jit(solution)/shard_map/ppermute | solution.py:291
  34.1 21.2 %collective-permute-start.10 = (bf16[8,256,128]{2,1,0:T(8,128)(2,1)S(1)}, bf16[8,256,128]{2,1,0:T(8,128)(2,1)S(1)}, u32[]{:S(2)}, u32[]{:S(2)}) collective-permute-start(bf16[8,256,128]{2,1,0:T(8,128)(2,1)S(1)} %get-tuple-element.38), channel_id=1, source_target_pairs={{0,8},{8,0},{16,24},{24,16},{1,9},{9,1},{17,25},{25,17},{2,10},{10... | collective-permute-start | bytes 1572872 | tf_op jit(solution)/shard_map/ppermute | solution.py:291
  34.1 7.1 %collective-permute-start.4 = (bf16[2,256,128]{2,1,0:T(8,128)(2,1)S(1)}, bf16[2,256,128]{2,1,0:T(8,128)(2,1)S(1)}, u32[]{:S(2)}, u32[]{:S(2)}) collective-permute-start(bf16[2,256,128]{2,1,0:T(8,128)(2,1)S(1)} %get-tuple-element.33), channel_id=1, source_target_pairs={{0,16},{8,24},{16,0},{24,8},{1,17},{9,25},{17,1},{25,9},{2,18},{10... | collective-permute-start | bytes 393224 | tf_op jit(solution)/shard_map/ppermute | solution.py:291
  38.5 9.2 %collective-permute-start.6 = (bf16[4,256,128]{2,1,0:T(8,128)(2,1)S(1)}, bf16[4,256,128]{2,1,0:T(8,128)(2,1)S(1)}, u32[]{:S(2)}, u32[]{:S(2)}) collective-permute-start(bf16[4,256,128]{2,1,0:T(8,128)(2,1)S(1)} %get-tuple-element.34), channel_id=1, source_target_pairs={{0,16},{8,24},{16,0},{24,8},{1,17},{9,25},{17,1},{25,9},{2,18},{10... | collective-permute-start | bytes 786440 | tf_op jit(solution)/shard_map/ppermute | solution.py:291
  41.3 12.0 %collective-permute-start.8 = (bf16[4,256,128]{2,1,0:T(8,128)(2,1)S(1)}, bf16[4,256,128]{2,1,0:T(8,128)(2,1)S(1)}, u32[]{:S(2)}, u32[]{:S(2)}) collective-permute-start(bf16[4,256,128]{2,1,0:T(8,128)(2,1)S(1)} %get-tuple-element.35), channel_id=1, source_target_pairs={{0,16},{8,24},{16,0},{24,8},{1,17},{9,25},{17,1},{25,9},{2,18},{10... | collective-permute-start | bytes 786440 | tf_op jit(solution)/shard_map/ppermute | solution.py:291
  47.7 11.2 %collective-permute-start.12 = (bf16[4,256,128]{2,1,0:T(8,128)(2,1)S(1)}, bf16[4,256,128]{2,1,0:T(8,128)(2,1)S(1)}, u32[]{:S(2)}, u32[]{:S(2)}) collective-permute-start(bf16[4,256,128]{2,1,0:T(8,128)(2,1)S(1)} %get-tuple-element.42.refs_0_), channel_id=1, source_target_pairs={{0,16},{8,24},{16,0},{24,8},{1,17},{9,25},{17,1},{25,9},{2,18},{10... | collective-permute-start | bytes 786440 | tf_op jit(solution)/shard_map/ppermute | solution.py:291
  49.7 14.8 %collective-permute-start.14 = (bf16[4,256,128]{2,1,0:T(8,128)(2,1)S(1)}, bf16[4,256,128]{2,1,0:T(8,128)(2,1)S(1)}, u32[]{:S(2)}, u32[]{:S(2)}) collective-permute-start(bf16[4,256,128]{2,1,0:T(8,128)(2,1)S(1)} %get-tuple-element.43), channel_id=1, source_target_pairs={{0,16},{8,24},{16,0},{24,8},{1,17},{9,25},{17,1},{25,9},{2,18},{10... | collective-permute-start | bytes 786440 | tf_op jit(solution)/shard_map/ppermute | solution.py:291
  53.3 16.9 %collective-permute-start.18 = (bf16[4,256,128]{2,1,0:T(8,128)(2,1)S(1)}, bf16[4,256,128]{2,1,0:T(8,128)(2,1)S(1)}, u32[]{:S(2)}, u32[]{:S(2)}) collective-permute-start(bf16[4,256,128]{2,1,0:T(8,128)(2,1)S(1)} %get-tuple-element.48), channel_id=1, source_target_pairs={{0,16},{8,24},{16,0},{24,8},{1,17},{9,25},{17,1},{25,9},{2,18},{10... | collective-permute-start | bytes 786440 | tf_op jit(solution)/shard_map/ppermute | solution.py:291
  55.3 19.2 %collective-permute-start.20 = (bf16[4,256,128]{2,1,0:T(8,128)(2,1)S(1)}, bf16[4,256,128]{2,1,0:T(8,128)(2,1)S(1)}, u32[]{:S(2)}, u32[]{:S(2)}) collective-permute-start(bf16[4,256,128]{2,1,0:T(8,128)(2,1)S(1)} %get-tuple-element.49), channel_id=1, source_target_pairs={{0,16},{8,24},{16,0},{24,8},{1,17},{9,25},{17,1},{25,9},{2,18},{10... | collective-permute-start | bytes 786440 | tf_op jit(solution)/shard_map/ppermute | solution.py:291
  58.9 37.2 %collective-permute-start.7 = (bf16[4,256,128]{2,1,0:T(8,128)(2,1)S(1)}, bf16[4,256,128]{2,1,0:T(8,128)(2,1)S(1)}, u32[]{:S(2)}, u32[]{:S(2)}) collective-permute-start(bf16[4,256,128]{2,1,0:T(8,128)(2,1)S(1)} %add_tiles.15), channel_id=1, source_target_pairs={{0,4},{1,5},{2,6},{3,7},{4,0},{5,1},{6,2},{7,3},{8,12},{9,13},{10,... | collective-permute-start | bytes 786440 | tf_op jit(solution)/shard_map/ppermute | solution.py:291
  64.5 35.3 %collective-permute-start.9 = (bf16[4,256,128]{2,1,0:T(8,128)(2,1)S(1)}, bf16[4,256,128]{2,1,0:T(8,128)(2,1)S(1)}, u32[]{:S(2)}, u32[]{:S(2)}) collective-permute-start(bf16[4,256,128]{2,1,0:T(8,128)(2,1)S(1)} %add_tiles.16), channel_id=1, source_target_pairs={{0,6},{1,7},{2,4},{3,5},{4,2},{5,3},{6,0},{7,1},{8,14},{9,15},{10,... | collective-permute-start | bytes 786440 | tf_op jit(solution)/shard_map/ppermute | solution.py:291
  68.8 24.2 %collective-permute-start.3 = (bf16[2,256,128]{2,1,0:T(8,128)(2,1)S(1)}, bf16[2,256,128]{2,1,0:T(8,128)(2,1)S(1)}, u32[]{:S(2)}, u32[]{:S(2)}) collective-permute-start(bf16[2,256,128]{2,1,0:T(8,128)(2,1)S(1)} %add_tiles.13), channel_id=1, source_target_pairs={{0,5},{1,4},{2,7},{3,6},{4,1},{5,0},{6,3},{7,2},{8,13},{9,12},{10,... | collective-permute-start | bytes 393224 | tf_op jit(solution)/shard_map/ppermute | solution.py:291
  70.1 24.5 %collective-permute-start.5 = (bf16[2,256,128]{2,1,0:T(8,128)(2,1)S(1)}, bf16[2,256,128]{2,1,0:T(8,128)(2,1)S(1)}, u32[]{:S(2)}, u32[]{:S(2)}) collective-permute-start(bf16[2,256,128]{2,1,0:T(8,128)(2,1)S(1)} %add_tiles.14), channel_id=1, source_target_pairs={{0,5},{1,4},{2,7},{3,6},{4,1},{5,0},{6,3},{7,2},{8,13},{9,12},{10,... | collective-permute-start | bytes 393224 | tf_op jit(solution)/shard_map/ppermute | solution.py:291
  74.4 29.1 %copy-start = (s32[8,8,4]{1,2,0:T(4,128)S(1)}, s32[8,8,4]{1,2,0:T(4,128)}, u32[]{:S(2)}) copy-start(s32[8,8,4]{1,2,0:T(4,128)} %param.9) | copy-start | bytes 3076
  74.6 25.3 %collective-permute-start.13 = (bf16[4,256,128]{2,1,0:T(8,128)(2,1)S(1)}, bf16[4,256,128]{2,1,0:T(8,128)(2,1)S(1)}, u32[]{:S(2)}, u32[]{:S(2)}) collective-permute-start(bf16[4,256,128]{2,1,0:T(8,128)(2,1)S(1)} %add_tiles.18), channel_id=1, source_target_pairs={{0,3},{1,2},{2,1},{3,0},{4,7},{5,6},{6,5},{7,4},{8,11},{9,10},{10,... | collective-permute-start | bytes 786440 | tf_op jit(solution)/shard_map/ppermute | solution.py:291
  92.9 10.6 %collective-permute-start.15 = (bf16[4,256,128]{2,1,0:T(8,128)(2,1)S(1)}, bf16[4,256,128]{2,1,0:T(8,128)(2,1)S(1)}, u32[]{:S(2)}, u32[]{:S(2)}) collective-permute-start(bf16[4,256,128]{2,1,0:T(8,128)(2,1)S(1)} %add_tiles.19), channel_id=1, source_target_pairs={{0,1},{1,0},{2,3},{3,2},{4,5},{5,4},{6,7},{7,6},{8,9},{9,8},{10,11... | collective-permute-start | bytes 786440 | tf_op jit(solution)/shard_map/ppermute | solution.py:291
  94.6 10.0 %collective-permute-start.22 = (bf16[4,256,128]{2,1,0:T(8,128)(2,1)S(1)}, bf16[4,256,128]{2,1,0:T(8,128)(2,1)S(1)}, u32[]{:S(2)}, u32[]{:S(2)}) collective-permute-start(bf16[4,256,128]{2,1,0:T(8,128)(2,1)S(1)} %get-tuple-element.50), channel_id=1, source_target_pairs={{0,16},{8,24},{16,0},{24,8},{1,17},{9,25},{17,1},{25,9},{2,18},{10... | collective-permute-start | bytes 786440 | tf_op jit(solution)/shard_map/ppermute | solution.py:291
  96.1 11.9 %collective-permute-start.19 = (bf16[4,256,128]{2,1,0:T(8,128)(2,1)S(1)}, bf16[4,256,128]{2,1,0:T(8,128)(2,1)S(1)}, u32[]{:S(2)}, u32[]{:S(2)}) collective-permute-start(bf16[4,256,128]{2,1,0:T(8,128)(2,1)S(1)} %add_tiles.21), channel_id=1, source_target_pairs={{0,7},{1,6},{2,5},{3,4},{4,3},{5,2},{6,1},{7,0},{8,15},{9,14},{10,... | collective-permute-start | bytes 786440 | tf_op jit(solution)/shard_map/ppermute | solution.py:291
  99.9 10.5 %collective-permute-start.21 = (bf16[4,256,128]{2,1,0:T(8,128)(2,1)S(1)}, bf16[4,256,128]{2,1,0:T(8,128)(2,1)S(1)}, u32[]{:S(2)}, u32[]{:S(2)}) collective-permute-start(bf16[4,256,128]{2,1,0:T(8,128)(2,1)S(1)} %add_tiles.22), channel_id=1, source_target_pairs={{0,2},{1,3},{2,0},{3,1},{4,6},{5,7},{6,4},{7,5},{8,10},{9,11},{10,... | collective-permute-start | bytes 786440 | tf_op jit(solution)/shard_map/ppermute | solution.py:291

commit v2 on v1

--- a/solution.py
+++ b/solution.py
@@ -16,7 +16,7 @@
 BLOCK = 256
 HALVES = 2
 SIDE = 64
-CHUNK_EDGES = (0, 2, 4, 8, 12, 16, 20, 24, 28, 32)
+CHUNK_EDGES = (0, 1, 4, 8, 12, 16, 20, 24, 26, 28, 32)
 STAGE_EDGES = (0, 12, 20, 32)
 LATE = 3
 
@@ -342,9 +342,9 @@
             part = mine if stop - start == b - a else mine[start - a : stop - a]
             part = swap(part, "table", distance) if distance else part
             parts.append((distance, start % capacity, part))
-    late = len(parts) - LATE
-    total = gather_tiles(place, slots, parts[:late], last=False)
-    return gather_tiles(place, slots, parts[late:], before=total)
+    last = len(parts) - 1
+    total = gather_tiles(place, slots, parts[: last - LATE] + parts[last:], last=False)
+    return gather_tiles(place, slots, parts[last - LATE : last], before=total)
 
 
 def solution(mesh):

time: 113 us -> 112 us (level)
  waiting for transfers between devices: 48.9 us -> 44.8 us
  starting transfers between devices: 33 us -> 36.9 us
    ppermute x23 -> x25, waiting for transfers between devices: 48.9 us -> 44.8 us  [swap(): lax.ppermute(array, axis, [(i, i ^ bit) for i in range(lax.axis_size(axis...]
    ppermute x23 -> x25, starting transfers between devices: 33 us -> 36.9 us  [swap(): lax.ppermute(array, axis, [(i, i ^ bit) for i in range(lax.axis_size(axis...]
  transfers between devices with their start and end apart: 23 -> 25, of which waited for: 14 -> 14; matrix products, arithmetic and copies ran while one was open for 0% -> 0% of each run, Pallas kernels for 6% -> 6%
where the time goes in v2:
time: 112 us
  waiting for transfers between devices  44.8 us (40%)
  starting transfers between devices  36.9 us (33%)
  Pallas kernels  30.3 us (27%)
    ppermute x25, waiting for transfers between devices, swap(): lax.ppermute(array, axis, [(i, i ^ bit) for i in range(lax.axis_size(axis...  44.8 us
    ppermute x25, starting transfers between devices, swap(): lax.ppermute(array, axis, [(i, i ^ bit) for i in range(lax.axis_size(axis...  36.9 us
    pallas_call x1, Pallas kernels, first_products(): pl.pallas_call(functools.partial(first_kernel, groups=groups), grid_spec=...  17.9 us
    pallas_call x2, Pallas kernels, rest_products(): pl.pallas_call(functools.partial(rest_kernel, count=replicas), grid_spec=...  7.87 us
    pallas_call x2, Pallas kernels, gather_tiles(): pl.pallas_call(functools.partial(gather_kernel, plan=tuple(((distance, at...  3.15 us
  transfers between devices with their start and end apart: 25, of which 14 were waited for; matrix products, arithmetic and copies ran while one was open for 0% of the time, Pallas kernels for 6%

profile of v2, /device:TPU:0, one launch (start us, length us, event | category | flops | bytes accessed | tf_op | source)
XLA Modules:
  0.0 112.3 jit_solution(17055128050208758891)
XLA Ops:
  0.1 17.9 %first_products.1 = (bf16[1024,4096]{1,0:T(8,128)(2,1)S(1)}, bf16[1024,1024]{1,0:T(8,128)(2,1)S(1)}, bf16[12,256,128]{2,1,0:T(8,128)(2,1)S(1)}, bf16[12,256,128]...) custom-call(s32[10]{0:T(128)S(1)} %stack.40.place_ref, f32[8]{0:T(128)} %scale_ref.1, ...), custom_call_target="tpu_custom_call" | custom-call | flops 8589934592 | bytes 16777216 | tf_op jit(solution)/shard_map/first_products/pallas_call | solution.py:130
  18.0 0.6 collective-permute-start.1
  18.6 1.9 %collective-permute-done.1.refs_0_ = bf16[12,256,128]{2,1,0:T(8,128)(2,1)S(1)} collective-permute-done((bf16[12,256,128]{2,1,0:T(8,128)(2,1)S(1)}, bf16[12,256,128]{2,1,0:T(8,128)(2,1)S(1)}, u32[]{:S(2)}, u32[]{:S(2)}) %collective-permute-start.1) | collective-permute-done | bytes 786464 | tf_op jit(solution)/shard_map/ppermute | solution.py:291
  20.5 0.2 add_tiles.13
  20.7 3.3 %rest_products.2 = (bf16[8,256,128]{2,1,0:T(8,128)(2,1)S(1)}, bf16[8,256,128]{2,1,0:T(8,128)(2,1)S(1)}, bf16[8,256,128]{2,1,0:T(8,128)(2,1)S(1)}, bf16[8,256,128]{2,1,0:T(8,128)(2,1)S(1)}) custom-call(s32[10]{0:T(128)S(1)} %stack.40.place_ref, bf16[1024,4096]{1,0:T(8,128)(2,1)S(1)} %get-tuple-element.37.coef_ref, ...), custom_call_target="tpu_custom_call" | custom-call | flops 2147483648 | bytes 6291456 | tf_op jit(solution)/shard_map/rest_products/pallas_call | solution.py:178
  24.0 0.4 collective-permute-start.11
  24.4 0.1 collective-permute-start
  24.5 1.4 %collective-permute-done.11.refs_0_ = bf16[8,256,128]{2,1,0:T(8,128)(2,1)S(1)} collective-permute-done((bf16[8,256,128]{2,1,0:T(8,128)(2,1)S(1)}, bf16[8,256,128]{2,1,0:T(8,128)(2,1)S(1)}, u32[]{:S(2)}, u32[]{:S(2)}) %collective-permute-start.11) | collective-permute-done | bytes 524320 | tf_op jit(solution)/shard_map/ppermute | solution.py:291
  25.9 0.1 add_tiles.18
  26.1 4.6 %rest_products.3 = (bf16[12,256,128]{2,1,0:T(8,128)(2,1)S(1)}, bf16[12,256,128]{2,1,0:T(8,128)(2,1)S(1)}, bf16[12,256,128]{2,1,0:T(8,128)(2,1)S(1)}, bf16[12,256,128]{2,1,0:T(8,128)(2,1)S(1)}) custom-call(s32[10]{0:T(128)S(1)} %stack.40.place_ref, bf16[1024,4096]{1,0:T(8,128)(2,1)S(1)} %get-tuple-element.37.coef_ref, ...), custom_call_target="tpu_custom_call" | custom-call | flops 3221225472 | bytes 8388608 | tf_op jit(solution)/shard_map/rest_products/pallas_call | solution.py:178
  30.7 0.4 collective-permute-start.17
  31.1 2.6 %collective-permute-start.2 = (bf16[1,256,128]{2,1,0:T(8,128)(2,1)S(1)}, bf16[1,256,128]{2,1,0:T(8,128)(2,1)S(1)}, u32[]{:S(2)}, u32[]{:S(2)}) collective-permute-start(bf16[1,256,128]{2,1,0:T(8,128)(2,1)S(1)} %get-tuple-element.33.refs_0_), channel_id=1, source_target_pairs={{0,16},{8,24},{16,0},{24,8},{1,17},{9,25},{17,1},{25,9},{2,18},{10... | collective-permute-start | bytes 196616 | tf_op jit(solution)/shard_map/ppermute | solution.py:291
  33.8 0.3 collective-permute-start.4
  34.1 2.2 %collective-permute-done.2.refs_2_ = bf16[1,256,128]{2,1,0:T(8,128)(2,1)S(1)} collective-permute-done((bf16[1,256,128]{2,1,0:T(8,128)(2,1)S(1)}, bf16[1,256,128]{2,1,0:T(8,128)(2,1)S(1)}, u32[]{:S(2)}, u32[]{:S(2)}) %collective-permute-start.2) | collective-permute-done | bytes 65568 | tf_op jit(solution)/shard_map/ppermute | solution.py:291
  36.4 3.9 %collective-permute-start.3 = (bf16[1,256,128]{2,1,0:T(8,128)(2,1)S(1)}, bf16[1,256,128]{2,1,0:T(8,128)(2,1)S(1)}, u32[]{:S(2)}, u32[]{:S(2)}) collective-permute-start(bf16[1,256,128]{2,1,0:T(8,128)(2,1)S(1)} %add_tiles.14), channel_id=1, source_target_pairs={{0,5},{1,4},{2,7},{3,6},{4,1},{5,0},{6,3},{7,2},{8,13},{9,12},{10,... | collective-permute-start | bytes 196616 | tf_op jit(solution)/shard_map/ppermute | solution.py:291
  40.3 2.1 %collective-permute-start.6 = (bf16[4,256,128]{2,1,0:T(8,128)(2,1)S(1)}, bf16[4,256,128]{2,1,0:T(8,128)(2,1)S(1)}, u32[]{:S(2)}, u32[]{:S(2)}) collective-permute-start(bf16[4,256,128]{2,1,0:T(8,128)(2,1)S(1)} %get-tuple-element.35), channel_id=1, source_target_pairs={{0,16},{8,24},{16,0},{24,8},{1,17},{9,25},{17,1},{25,9},{2,18},{10... | collective-permute-start | bytes 786440 | tf_op jit(solution)/shard_map/ppermute | solution.py:291
  42.4 0.7 collective-permute-done.3.refs_0_
  43.1 1.8 %collective-permute-start.8 = (bf16[4,256,128]{2,1,0:T(8,128)(2,1)S(1)}, bf16[4,256,128]{2,1,0:T(8,128)(2,1)S(1)}, u32[]{:S(2)}, u32[]{:S(2)}) collective-permute-start(bf16[4,256,128]{2,1,0:T(8,128)(2,1)S(1)} %get-tuple-element.36), channel_id=1, source_target_pairs={{0,16},{8,24},{16,0},{24,8},{1,17},{9,25},{17,1},{25,9},{2,18},{10... | collective-permute-start | bytes 786440 | tf_op jit(solution)/shard_map/ppermute | solution.py:291
  45.0 4.6 %collective-permute-done.6.refs_2_ = bf16[4,256,128]{2,1,0:T(8,128)(2,1)S(1)} collective-permute-done((bf16[4,256,128]{2,1,0:T(8,128)(2,1)S(1)}, bf16[4,256,128]{2,1,0:T(8,128)(2,1)S(1)}, u32[]{:S(2)}, u32[]{:S(2)}) %collective-permute-start.6) | collective-permute-done | bytes 262176 | tf_op jit(solution)/shard_map/ppermute | solution.py:291
  49.5 1.3 %collective-permute-start.5 = (bf16[3,256,128]{2,1,0:T(8,128)(2,1)S(1)}, bf16[3,256,128]{2,1,0:T(8,128)(2,1)S(1)}, u32[]{:S(2)}, u32[]{:S(2)}) collective-permute-start(bf16[3,256,128]{2,1,0:T(8,128)(2,1)S(1)} %add_tiles.15), channel_id=1, source_target_pairs={{0,5},{1,4},{2,7},{3,6},{4,1},{5,0},{6,3},{7,2},{8,13},{9,12},{10,... | collective-permute-start | bytes 589832 | tf_op jit(solution)/shard_map/ppermute | solution.py:291
  50.8 0.1 add_tiles.16
  50.9 2.5 %collective-permute-done.8.refs_2_ = bf16[4,256,128]{2,1,0:T(8,128)(2,1)S(1)} collective-permute-done((bf16[4,256,128]{2,1,0:T(8,128)(2,1)S(1)}, bf16[4,256,128]{2,1,0:T(8,128)(2,1)S(1)}, u32[]{:S(2)}, u32[]{:S(2)}) %collective-permute-start.8) | collective-permute-done | bytes 262176 | tf_op jit(solution)/shard_map/ppermute | solution.py:291
  53.4 1.5 %collective-permute-start.7 = (bf16[4,256,128]{2,1,0:T(8,128)(2,1)S(1)}, bf16[4,256,128]{2,1,0:T(8,128)(2,1)S(1)}, u32[]{:S(2)}, u32[]{:S(2)}) collective-permute-start(bf16[4,256,128]{2,1,0:T(8,128)(2,1)S(1)} %add_tiles.16), channel_id=1, source_target_pairs={{0,4},{1,5},{2,6},{3,7},{4,0},{5,1},{6,2},{7,3},{8,12},{9,13},{10,... | collective-permute-start | bytes 786440 | tf_op jit(solution)/shard_map/ppermute | solution.py:291
  54.9 10.8 %collective-permute-done.5.refs_1_ = bf16[3,256,128]{2,1,0:T(8,128)(2,1)S(1)} collective-permute-done((bf16[3,256,128]{2,1,0:T(8,128)(2,1)S(1)}, bf16[3,256,128]{2,1,0:T(8,128)(2,1)S(1)}, u32[]{:S(2)}, u32[]{:S(2)}) %collective-permute-start.5) | collective-permute-done | bytes 196640 | tf_op jit(solution)/shard_map/ppermute | solution.py:291
  65.7 2.5 %collective-permute-start.12 = (bf16[4,256,128]{2,1,0:T(8,128)(2,1)S(1)}, bf16[4,256,128]{2,1,0:T(8,128)(2,1)S(1)}, u32[]{:S(2)}, u32[]{:S(2)}) collective-permute-start(bf16[4,256,128]{2,1,0:T(8,128)(2,1)S(1)} %get-tuple-element.43.refs_0_), channel_id=1, source_target_pairs={{0,16},{8,24},{16,0},{24,8},{1,17},{9,25},{17,1},{25,9},{2,18},{10... | collective-permute-start | bytes 786440 | tf_op jit(solution)/shard_map/ppermute | solution.py:291
  68.3 0.2 add_tiles.21
  68.5 1.2 %collective-permute-done.7.refs_2_ = bf16[4,256,128]{2,1,0:T(8,128)(2,1)S(1)} collective-permute-done((bf16[4,256,128]{2,1,0:T(8,128)(2,1)S(1)}, bf16[4,256,128]{2,1,0:T(8,128)(2,1)S(1)}, u32[]{:S(2)}, u32[]{:S(2)}) %collective-permute-start.7) | collective-permute-done | bytes 262176 | tf_op jit(solution)/shard_map/ppermute | solution.py:291
  69.6 1.7 %collective-permute-start.19 = (bf16[4,256,128]{2,1,0:T(8,128)(2,1)S(1)}, bf16[4,256,128]{2,1,0:T(8,128)(2,1)S(1)}, u32[]{:S(2)}, u32[]{:S(2)}) collective-permute-start(bf16[4,256,128]{2,1,0:T(8,128)(2,1)S(1)} %get-tuple-element.50), channel_id=1, source_target_pairs={{0,16},{8,24},{16,0},{24,8},{1,17},{9,25},{17,1},{25,9},{2,18},{10... | collective-permute-start | bytes 786440 | tf_op jit(solution)/shard_map/ppermute | solution.py:291
  71.4 0.1 add_tiles.17
  71.5 0.3 collective-permute-start.21
  71.8 2.7 %collective-permute-done.12.refs_2_ = bf16[4,256,128]{2,1,0:T(8,128)(2,1)S(1)} collective-permute-done((bf16[4,256,128]{2,1,0:T(8,128)(2,1)S(1)}, bf16[4,256,128]{2,1,0:T(8,128)(2,1)S(1)}, u32[]{:S(2)}, u32[]{:S(2)}) %collective-permute-start.12) | collective-permute-done | bytes 262176 | tf_op jit(solution)/shard_map/ppermute | solution.py:291
  74.6 2.8 %collective-permute-start.9 = (bf16[4,256,128]{2,1,0:T(8,128)(2,1)S(1)}, bf16[4,256,128]{2,1,0:T(8,128)(2,1)S(1)}, u32[]{:S(2)}, u32[]{:S(2)}) collective-permute-start(bf16[4,256,128]{2,1,0:T(8,128)(2,1)S(1)} %add_tiles.17), channel_id=1, source_target_pairs={{0,6},{1,7},{2,4},{3,5},{4,2},{5,3},{6,0},{7,1},{8,14},{9,15},{10,... | collective-permute-start | bytes 786440 | tf_op jit(solution)/shard_map/ppermute | solution.py:291
  77.4 2.8 %collective-permute-done.14.refs_2_ = bf16[4,256,128]{2,1,0:T(8,128)(2,1)S(1)} collective-permute-done((bf16[4,256,128]{2,1,0:T(8,128)(2,1)S(1)}, bf16[4,256,128]{2,1,0:T(8,128)(2,1)S(1)}, u32[]{:S(2)}, u32[]{:S(2)}) %collective-permute-start.14) | collective-permute-done | bytes 262176 | tf_op jit(solution)/shard_map/ppermute | solution.py:291
  80.2 2.5 %collective-permute-start.18 = (bf16[4,256,128]{2,1,0:T(8,128)(2,1)S(1)}, bf16[4,256,128]{2,1,0:T(8,128)(2,1)S(1)}, u32[]{:S(2)}, u32[]{:S(2)}) collective-permute-start(bf16[4,256,128]{2,1,0:T(8,128)(2,1)S(1)} %get-tuple-element.49), channel_id=1, source_target_pairs={{0,16},{8,24},{16,0},{24,8},{1,17},{9,25},{17,1},{25,9},{2,18},{10... | collective-permute-start | bytes 786440 | tf_op jit(solution)/shard_map/ppermute | solution.py:291
  82.7 0.1 add_tiles.19
  82.8 0.1 add_tiles.20
  82.9 5.1 %collective-permute-done.21.refs_2_ = bf16[2,256,128]{2,1,0:T(8,128)(2,1)S(1)} collective-permute-done((bf16[2,256,128]{2,1,0:T(8,128)(2,1)S(1)}, bf16[2,256,128]{2,1,0:T(8,128)(2,1)S(1)}, u32[]{:S(2)}, u32[]{:S(2)}) %collective-permute-start.21) | collective-permute-done | bytes 131104 | tf_op jit(solution)/shard_map/ppermute | solution.py:291
  88.1 0.6 collective-permute-start.13
  88.7 1.5 %collective-permute-start.15 = (bf16[4,256,128]{2,1,0:T(8,128)(2,1)S(1)}, bf16[4,256,128]{2,1,0:T(8,128)(2,1)S(1)}, u32[]{:S(2)}, u32[]{:S(2)}) collective-permute-start(bf16[4,256,128]{2,1,0:T(8,128)(2,1)S(1)} %add_tiles.20), channel_id=1, source_target_pairs={{0,1},{1,0},{2,3},{3,2},{4,5},{5,4},{6,7},{7,6},{8,9},{9,8},{10,11... | collective-permute-start | bytes 786440 | tf_op jit(solution)/shard_map/ppermute | solution.py:291
  90.2 0.1 add_tiles.23
  90.3 2.0 %collective-permute-done.23.refs_2_ = bf16[2,256,128]{2,1,0:T(8,128)(2,1)S(1)} collective-permute-done((bf16[2,256,128]{2,1,0:T(8,128)(2,1)S(1)}, bf16[2,256,128]{2,1,0:T(8,128)(2,1)S(1)}, u32[]{:S(2)}, u32[]{:S(2)}) %collective-permute-start.23) | collective-permute-done | bytes 131104 | tf_op jit(solution)/shard_map/ppermute | solution.py:291
  92.3 7.6 %collective-permute-start.20 = (bf16[4,256,128]{2,1,0:T(8,128)(2,1)S(1)}, bf16[4,256,128]{2,1,0:T(8,128)(2,1)S(1)}, u32[]{:S(2)}, u32[]{:S(2)}) collective-permute-start(bf16[4,256,128]{2,1,0:T(8,128)(2,1)S(1)} %add_tiles.23), channel_id=1, source_target_pairs={{0,7},{1,6},{2,5},{3,4},{4,3},{5,2},{6,1},{7,0},{8,15},{9,14},{10,... | collective-permute-start | bytes 786440 | tf_op jit(solution)/shard_map/ppermute | solution.py:291
  100.1 2.0 %collective-permute-start.24 = (bf16[2,256,128]{2,1,0:T(8,128)(2,1)S(1)}, bf16[2,256,128]{2,1,0:T(8,128)(2,1)S(1)}, u32[]{:S(2)}, u32[]{:S(2)}) collective-permute-start(bf16[2,256,128]{2,1,0:T(8,128)(2,1)S(1)} %add_tiles.25), channel_id=1, source_target_pairs={{0,2},{1,3},{2,0},{3,1},{4,6},{5,7},{6,4},{7,5},{8,10},{9,11},{10,... | collective-permute-start | bytes 393224 | tf_op jit(solution)/shard_map/ppermute | solution.py:291
  102.1 0.1 add_tiles.22.refs_6_
  102.2 1.2 %gather_tiles.2.refs_0_ = f32[8,256,128]{2,1,0:T(8,128)S(1)} custom-call(s32[10]{0:T(128)S(1)} %stack.40.place_ref, s32[8,4,8]{2,1,0:T(4,128)S(1)} %bitcast.16, bf16[1,256,128]{2,1,0:T(8,128)(2,1)S(1)} %collective-permute-done.3.refs_0_, bf16[3,256,128]{2,1,0:T(8,128)(2,1)S(1)} %collective-permute-done.5.refs_1_, ...), custom_call_target="tpu_custom_call" | custom-call | tf_op jit(solution)/shard_map/gather_tiles/pallas_call | solution.py:263
  103.4 5.5 %collective-permute-done.22.refs_2_ = bf16[2,256,128]{2,1,0:T(8,128)(2,1)S(1)} collective-permute-done((bf16[2,256,128]{2,1,0:T(8,128)(2,1)S(1)}, bf16[2,256,128]{2,1,0:T(8,128)(2,1)S(1)}, u32[]{:S(2)}, u32[]{:S(2)}) %collective-permute-start.22) | collective-permute-done | bytes 131104 | tf_op jit(solution)/shard_map/ppermute | solution.py:291
  108.9 1.4 %collective-permute-done.24.refs_3_ = bf16[2,256,128]{2,1,0:T(8,128)(2,1)S(1)} collective-permute-done((bf16[2,256,128]{2,1,0:T(8,128)(2,1)S(1)}, bf16[2,256,128]{2,1,0:T(8,128)(2,1)S(1)}, u32[]{:S(2)}, u32[]{:S(2)}) %collective-permute-start.24) | collective-permute-done | bytes 131104 | tf_op jit(solution)/shard_map/ppermute | solution.py:291
  110.3 2.0 %gather_tiles.3 = bf16[1024,256]{1,0:T(8,128)(2,1)} custom-call(s32[10]{0:T(128)S(1)} %stack.40.place_ref, s32[8,4,8]{2,1,0:T(4,128)S(1)} %bitcast.17, f32[8,256,128]{2,1,0:T(8,128)S(1)} %gather_tiles.2.refs_0_, bf16[4,256,128]{2,1,0:T(8,128)(2,1)S(1)} %collective-permute-done.20.refs_1_, bf16[2,256,128]{2,1,0:T(8,128)(2,1)S(1)} %collective-permute-done.22.refs_2_, ...), custom_call_target="tpu_custom_call" | custom-call | tf_op jit(solution)/shard_map/gather_tiles/pallas_call | solution.py:263
  (23 shorter events, 0.5 us)
Async XLA Ops:
  18.0 2.5 %collective-permute-start.1 = (bf16[12,256,128]{2,1,0:T(8,128)(2,1)S(1)}, bf16[12,256,128]{2,1,0:T(8,128)(2,1)S(1)}, u32[]{:S(2)}, u32[]{:S(2)}) collective-permute-start(bf16[12,256,128]{2,1,0:T(8,128)(2,1)S(1)} %get-tuple-element.31), channel_id=1, source_target_pairs={{0,8},{8,0},{16,24},{24,16},{1,9},{9,1},{17,25},{25,17},{2,10},{10... | collective-permute-start | bytes 2359304 | tf_op jit(solution)/shard_map/ppermute | solution.py:291
  24.0 2.0 %collective-permute-start.11 = (bf16[8,256,128]{2,1,0:T(8,128)(2,1)S(1)}, bf16[8,256,128]{2,1,0:T(8,128)(2,1)S(1)}, u32[]{:S(2)}, u32[]{:S(2)}) collective-permute-start(bf16[8,256,128]{2,1,0:T(8,128)(2,1)S(1)} %get-tuple-element.41), channel_id=1, source_target_pairs={{0,8},{8,0},{16,24},{24,16},{1,9},{9,1},{17,25},{25,17},{2,10},{10... | collective-permute-start | bytes 1572872 | tf_op jit(solution)/shard_map/ppermute | solution.py:291
  24.4 9.7 %collective-permute-start = (bf16[12,256,128]{2,1,0:T(8,128)(2,1)S(1)}, bf16[12,256,128]{2,1,0:T(8,128)(2,1)S(1)}, u32[]{:S(2)}, u32[]{:S(2)}) collective-permute-start(bf16[12,256,128]{2,1,0:T(8,128)(2,1)S(1)} %get-tuple-element.29), channel_id=1, source_target_pairs={{0,8},{8,0},{16,24},{24,16},{1,9},{9,1},{17,25},{25,17},{2,10},{10... | collective-permute-start | bytes 2359304 | tf_op jit(solution)/shard_map/ppermute | solution.py:291
  30.7 37.6 %collective-permute-start.17 = (bf16[12,256,128]{2,1,0:T(8,128)(2,1)S(1)}, bf16[12,256,128]{2,1,0:T(8,128)(2,1)S(1)}, u32[]{:S(2)}, u32[]{:S(2)}) collective-permute-start(bf16[12,256,128]{2,1,0:T(8,128)(2,1)S(1)} %get-tuple-element.47), channel_id=1, source_target_pairs={{0,8},{8,0},{16,24},{24,16},{1,9},{9,1},{17,25},{25,17},{2,10},{10... | collective-permute-start | bytes 2359304 | tf_op jit(solution)/shard_map/ppermute | solution.py:291
  31.1 5.2 %collective-permute-start.2 = (bf16[1,256,128]{2,1,0:T(8,128)(2,1)S(1)}, bf16[1,256,128]{2,1,0:T(8,128)(2,1)S(1)}, u32[]{:S(2)}, u32[]{:S(2)}) collective-permute-start(bf16[1,256,128]{2,1,0:T(8,128)(2,1)S(1)} %get-tuple-element.33.refs_0_), channel_id=1, source_target_pairs={{0,16},{8,24},{16,0},{24,8},{1,17},{9,25},{17,1},{25,9},{2,18},{10... | collective-permute-start | bytes 196616 | tf_op jit(solution)/shard_map/ppermute | solution.py:291
  33.8 48.9 %collective-permute-start.16 = (bf16[12,256,128]{2,1,0:T(8,128)(2,1)S(1)}, bf16[12,256,128]{2,1,0:T(8,128)(2,1)S(1)}, u32[]{:S(2)}, u32[]{:S(2)}) collective-permute-start(bf16[12,256,128]{2,1,0:T(8,128)(2,1)S(1)} %get-tuple-element.45), channel_id=1, source_target_pairs={{0,8},{8,0},{16,24},{24,16},{1,9},{9,1},{17,25},{25,17},{2,10},{10... | collective-permute-start | bytes 2359304 | tf_op jit(solution)/shard_map/ppermute | solution.py:291
  33.8 11.0 %collective-permute-start.4 = (bf16[3,256,128]{2,1,0:T(8,128)(2,1)S(1)}, bf16[3,256,128]{2,1,0:T(8,128)(2,1)S(1)}, u32[]{:S(2)}, u32[]{:S(2)}) collective-permute-start(bf16[3,256,128]{2,1,0:T(8,128)(2,1)S(1)} %get-tuple-element.34), channel_id=1, source_target_pairs={{0,16},{8,24},{16,0},{24,8},{1,17},{9,25},{17,1},{25,9},{2,18},{10... | collective-permute-start | bytes 589832 | tf_op jit(solution)/shard_map/ppermute | solution.py:291
  36.4 6.7 %collective-permute-start.3 = (bf16[1,256,128]{2,1,0:T(8,128)(2,1)S(1)}, bf16[1,256,128]{2,1,0:T(8,128)(2,1)S(1)}, u32[]{:S(2)}, u32[]{:S(2)}) collective-permute-start(bf16[1,256,128]{2,1,0:T(8,128)(2,1)S(1)} %add_tiles.14), channel_id=1, source_target_pairs={{0,5},{1,4},{2,7},{3,6},{4,1},{5,0},{6,3},{7,2},{8,13},{9,12},{10,... | collective-permute-start | bytes 196616 | tf_op jit(solution)/shard_map/ppermute | solution.py:291
  40.3 9.2 %collective-permute-start.6 = (bf16[4,256,128]{2,1,0:T(8,128)(2,1)S(1)}, bf16[4,256,128]{2,1,0:T(8,128)(2,1)S(1)}, u32[]{:S(2)}, u32[]{:S(2)}) collective-permute-start(bf16[4,256,128]{2,1,0:T(8,128)(2,1)S(1)} %get-tuple-element.35), channel_id=1, source_target_pairs={{0,16},{8,24},{16,0},{24,8},{1,17},{9,25},{17,1},{25,9},{2,18},{10... | collective-permute-start | bytes 786440 | tf_op jit(solution)/shard_map/ppermute | solution.py:291
  43.1 10.3 %collective-permute-start.8 = (bf16[4,256,128]{2,1,0:T(8,128)(2,1)S(1)}, bf16[4,256,128]{2,1,0:T(8,128)(2,1)S(1)}, u32[]{:S(2)}, u32[]{:S(2)}) collective-permute-start(bf16[4,256,128]{2,1,0:T(8,128)(2,1)S(1)} %get-tuple-element.36), channel_id=1, source_target_pairs={{0,16},{8,24},{16,0},{24,8},{1,17},{9,25},{17,1},{25,9},{2,18},{10... | collective-permute-start | bytes 786440 | tf_op jit(solution)/shard_map/ppermute | solution.py:291
  44.9 26.6 %collective-permute-start.10 = (bf16[8,256,128]{2,1,0:T(8,128)(2,1)S(1)}, bf16[8,256,128]{2,1,0:T(8,128)(2,1)S(1)}, u32[]{:S(2)}, u32[]{:S(2)}) collective-permute-start(bf16[8,256,128]{2,1,0:T(8,128)(2,1)S(1)} %get-tuple-element.39), channel_id=1, source_target_pairs={{0,8},{8,0},{16,24},{24,16},{1,9},{9,1},{17,25},{25,17},{2,10},{10... | collective-permute-start | bytes 1572872 | tf_op jit(solution)/shard_map/ppermute | solution.py:291
  49.5 16.2 %collective-permute-start.5 = (bf16[3,256,128]{2,1,0:T(8,128)(2,1)S(1)}, bf16[3,256,128]{2,1,0:T(8,128)(2,1)S(1)}, u32[]{:S(2)}, u32[]{:S(2)}) collective-permute-start(bf16[3,256,128]{2,1,0:T(8,128)(2,1)S(1)} %add_tiles.15), channel_id=1, source_target_pairs={{0,5},{1,4},{2,7},{3,6},{4,1},{5,0},{6,3},{7,2},{8,13},{9,12},{10,... | collective-permute-start | bytes 589832 | tf_op jit(solution)/shard_map/ppermute | solution.py:291
  53.4 16.3 %collective-permute-start.7 = (bf16[4,256,128]{2,1,0:T(8,128)(2,1)S(1)}, bf16[4,256,128]{2,1,0:T(8,128)(2,1)S(1)}, u32[]{:S(2)}, u32[]{:S(2)}) collective-permute-start(bf16[4,256,128]{2,1,0:T(8,128)(2,1)S(1)} %add_tiles.16), channel_id=1, source_target_pairs={{0,4},{1,5},{2,6},{3,7},{4,0},{5,1},{6,2},{7,3},{8,12},{9,13},{10,... | collective-permute-start | bytes 786440 | tf_op jit(solution)/shard_map/ppermute | solution.py:291
  65.7 8.9 %collective-permute-start.12 = (bf16[4,256,128]{2,1,0:T(8,128)(2,1)S(1)}, bf16[4,256,128]{2,1,0:T(8,128)(2,1)S(1)}, u32[]{:S(2)}, u32[]{:S(2)}) collective-permute-start(bf16[4,256,128]{2,1,0:T(8,128)(2,1)S(1)} %get-tuple-element.43.refs_0_), channel_id=1, source_target_pairs={{0,16},{8,24},{16,0},{24,8},{1,17},{9,25},{17,1},{25,9},{2,18},{10... | collective-permute-start | bytes 786440 | tf_op jit(solution)/shard_map/ppermute | solution.py:291
  68.3 12.0 %collective-permute-start.14 = (bf16[4,256,128]{2,1,0:T(8,128)(2,1)S(1)}, bf16[4,256,128]{2,1,0:T(8,128)(2,1)S(1)}, u32[]{:S(2)}, u32[]{:S(2)}) collective-permute-start(bf16[4,256,128]{2,1,0:T(8,128)(2,1)S(1)} %get-tuple-element.44), channel_id=1, source_target_pairs={{0,16},{8,24},{16,0},{24,8},{1,17},{9,25},{17,1},{25,9},{2,18},{10... | collective-permute-start | bytes 786440 | tf_op jit(solution)/shard_map/ppermute | solution.py:291
  69.6 19.0 %collective-permute-start.19 = (bf16[4,256,128]{2,1,0:T(8,128)(2,1)S(1)}, bf16[4,256,128]{2,1,0:T(8,128)(2,1)S(1)}, u32[]{:S(2)}, u32[]{:S(2)}) collective-permute-start(bf16[4,256,128]{2,1,0:T(8,128)(2,1)S(1)} %get-tuple-element.50), channel_id=1, source_target_pairs={{0,16},{8,24},{16,0},{24,8},{1,17},{9,25},{17,1},{25,9},{2,18},{10... | collective-permute-start | bytes 786440 | tf_op jit(solution)/shard_map/ppermute | solution.py:291
  71.5 16.6 %collective-permute-start.21 = (bf16[2,256,128]{2,1,0:T(8,128)(2,1)S(1)}, bf16[2,256,128]{2,1,0:T(8,128)(2,1)S(1)}, u32[]{:S(2)}, u32[]{:S(2)}) collective-permute-start(bf16[2,256,128]{2,1,0:T(8,128)(2,1)S(1)} %get-tuple-element.51), channel_id=1, source_target_pairs={{0,16},{8,24},{16,0},{24,8},{1,17},{9,25},{17,1},{25,9},{2,18},{10... | collective-permute-start | bytes 393224 | tf_op jit(solution)/shard_map/ppermute | solution.py:291
  74.6 25.4 %collective-permute-start.9 = (bf16[4,256,128]{2,1,0:T(8,128)(2,1)S(1)}, bf16[4,256,128]{2,1,0:T(8,128)(2,1)S(1)}, u32[]{:S(2)}, u32[]{:S(2)}) collective-permute-start(bf16[4,256,128]{2,1,0:T(8,128)(2,1)S(1)} %add_tiles.17), channel_id=1, source_target_pairs={{0,6},{1,7},{2,4},{3,5},{4,2},{5,3},{6,0},{7,1},{8,14},{9,15},{10,... | collective-permute-start | bytes 786440 | tf_op jit(solution)/shard_map/ppermute | solution.py:291
  80.2 19.8 %collective-permute-start.18 = (bf16[4,256,128]{2,1,0:T(8,128)(2,1)S(1)}, bf16[4,256,128]{2,1,0:T(8,128)(2,1)S(1)}, u32[]{:S(2)}, u32[]{:S(2)}) collective-permute-start(bf16[4,256,128]{2,1,0:T(8,128)(2,1)S(1)} %get-tuple-element.49), channel_id=1, source_target_pairs={{0,16},{8,24},{16,0},{24,8},{1,17},{9,25},{17,1},{25,9},{2,18},{10... | collective-permute-start | bytes 786440 | tf_op jit(solution)/shard_map/ppermute | solution.py:291
  82.7 9.6 %collective-permute-start.23 = (bf16[2,256,128]{2,1,0:T(8,128)(2,1)S(1)}, bf16[2,256,128]{2,1,0:T(8,128)(2,1)S(1)}, u32[]{:S(2)}, u32[]{:S(2)}) collective-permute-start(bf16[2,256,128]{2,1,0:T(8,128)(2,1)S(1)} %get-tuple-element.52), channel_id=1, source_target_pairs={{0,16},{8,24},{16,0},{24,8},{1,17},{9,25},{17,1},{25,9},{2,18},{10... | collective-permute-start | bytes 393224 | tf_op jit(solution)/shard_map/ppermute | solution.py:291
  88.1 14.1 %collective-permute-start.13 = (bf16[4,256,128]{2,1,0:T(8,128)(2,1)S(1)}, bf16[4,256,128]{2,1,0:T(8,128)(2,1)S(1)}, u32[]{:S(2)}, u32[]{:S(2)}) collective-permute-start(bf16[4,256,128]{2,1,0:T(8,128)(2,1)S(1)} %add_tiles.19), channel_id=1, source_target_pairs={{0,3},{1,2},{2,1},{3,0},{4,7},{5,6},{6,5},{7,4},{8,11},{9,10},{10,... | collective-permute-start | bytes 786440 | tf_op jit(solution)/shard_map/ppermute | solution.py:291
  88.7 13.5 %collective-permute-start.15 = (bf16[4,256,128]{2,1,0:T(8,128)(2,1)S(1)}, bf16[4,256,128]{2,1,0:T(8,128)(2,1)S(1)}, u32[]{:S(2)}, u32[]{:S(2)}) collective-permute-start(bf16[4,256,128]{2,1,0:T(8,128)(2,1)S(1)} %add_tiles.20), channel_id=1, source_target_pairs={{0,1},{1,0},{2,3},{3,2},{4,5},{5,4},{6,7},{7,6},{8,9},{9,8},{10,11... | collective-permute-start | bytes 786440 | tf_op jit(solution)/shard_map/ppermute | solution.py:291
  92.3 18.0 %collective-permute-start.20 = (bf16[4,256,128]{2,1,0:T(8,128)(2,1)S(1)}, bf16[4,256,128]{2,1,0:T(8,128)(2,1)S(1)}, u32[]{:S(2)}, u32[]{:S(2)}) collective-permute-start(bf16[4,256,128]{2,1,0:T(8,128)(2,1)S(1)} %add_tiles.23), channel_id=1, source_target_pairs={{0,7},{1,6},{2,5},{3,4},{4,3},{5,2},{6,1},{7,0},{8,15},{9,14},{10,... | collective-permute-start | bytes 786440 | tf_op jit(solution)/shard_map/ppermute | solution.py:291
  99.9 2.3 %copy-start = (s32[8,8,4]{1,2,0:T(4,128)S(1)}, s32[8,8,4]{1,2,0:T(4,128)}, u32[]{:S(2)}) copy-start(s32[8,8,4]{1,2,0:T(4,128)} %param.9) | copy-start | bytes 3076
  100.0 8.9 %collective-permute-start.22 = (bf16[2,256,128]{2,1,0:T(8,128)(2,1)S(1)}, bf16[2,256,128]{2,1,0:T(8,128)(2,1)S(1)}, u32[]{:S(2)}, u32[]{:S(2)}) collective-permute-start(bf16[2,256,128]{2,1,0:T(8,128)(2,1)S(1)} %add_tiles.24), channel_id=1, source_target_pairs={{0,2},{1,3},{2,0},{3,1},{4,6},{5,7},{6,4},{7,5},{8,10},{9,11},{10,... | collective-permute-start | bytes 393224 | tf_op jit(solution)/shard_map/ppermute | solution.py:291
  100.1 10.2 %collective-permute-start.24 = (bf16[2,256,128]{2,1,0:T(8,128)(2,1)S(1)}, bf16[2,256,128]{2,1,0:T(8,128)(2,1)S(1)}, u32[]{:S(2)}, u32[]{:S(2)}) collective-permute-start(bf16[2,256,128]{2,1,0:T(8,128)(2,1)S(1)} %add_tiles.25), channel_id=1, source_target_pairs={{0,2},{1,3},{2,0},{3,1},{4,6},{5,7},{6,4},{7,5},{8,10},{9,11},{10,... | collective-permute-start | bytes 393224 | tf_op jit(solution)/shard_map/ppermute | solution.py:291
